TPU v7x, 32 devices: a whole 2x2x4 slice. The times are simulated.
32 devices in a mesh: obs: 4 (over y, x), patch: 8 (over z, core).
Axes of the slice: x: 2, y: 2, z: 4, core: 2. Of those that a mesh axis runs over, the one named last changes fastest.
Arguments:
- green: float32 [5120, 5120], P('obs', 'patch'), may hold values from -0.078125 to 0.078125
- data: float32 [5120, 128], P('obs'), may hold values from -6 to 6
- neighbours: int32 [3, 5120], P(None, 'patch'), may hold values from 0 to 5119, as said below
- reg_weight: float32 [128], replicated, may hold values from 0.5 to 2
Outputs:
- slip: float32 [5120, 128], P('patch')
Inputs may be any that keep to these rules, and one draw needn't show every extreme that they name: `neighbours`: entry (k, i) is a patch within 128 of i; an entry equal to i is padding. Distance 128 is reached in every draw.
All inputs are finite; a program needn't handle non-finite values.
Results may differ from a plain program's by a relative error of at most 0.0001.
Values sent between devices are 32-bit elements; how exact they have to be, the bound alone decides.
A program may use at most 64 MiB of HBM per device.

v0:
```python
import functools
import math

import jax
import jax.numpy as jnp
from jax import lax
from jax.experimental import pallas as pl
from jax.experimental.pallas import tpu as pltpu
from jax.sharding import PartitionSpec as P

BAND = 128
ITERS = 3
MESH = pl.DeviceIdType.MESH
F32 = jnp.float32
BF16 = jnp.bfloat16


def dot(a, b):
    return lax.dot_general(a, b, (((1,), (0,)), ((), ())), preferred_element_type=F32)


def split(x):
    hi = x.astype(BF16)
    return hi, (x - hi.astype(F32)).astype(BF16)


def kernel(n_obs, n_patch, nc, bc, green, data, nb, rw, out,
           ghi, glo, gthi, gtlo, lm, lmt, cat_d, cat_r, cat_e,
           d, g, a, wext, slip, sq, hd, hg, qd, qg,
           pf, s, rd, sr, sl, rl, rr, img, bb, br, hal, wr, scs, scr, pls, plr,
           sem_d, sem_l, sem_r, sem_i, sem_b, sem_h, sem_w, sem_s, sem_p, sem_n):
    rows, cols = green.shape
    E = data.shape[1]
    R = rows // 2 // nc
    BR = cols // bc
    half = rows // 2
    per = 4
    lag = 4
    CB = cols // BAND
    nz = n_patch // 2
    nbit = n_obs.bit_length() - 1
    obs = lax.axis_index("obs")
    pat = lax.axis_index("patch")
    z = pat // 2
    c = pat % 2
    other = 1 - c
    partner = z * 2 + other
    has_l, has_r = pat > 0, pat < n_patch - 1
    up, down = z < nz - 1, z > 0
    weight = rw[...]

    def at(o, q):
        return (o, q)

    def rcopy(src, dst, sems, dev):
        return pltpu.make_async_remote_copy(
            src_ref=src, dst_ref=dst, send_sem=sems[0], recv_sem=sems[1],
            device_id=dev, device_id_type=MESH)

    def pair(sem, *idx):
        return sem.at[(0,) + idx], sem.at[(1,) + idx]

    barrier = pltpu.get_barrier_semaphore()

    @pl.loop(1, n_patch)
    def _(i):
        pl.semaphore_signal(barrier, inc=1, device_id=at(obs, (pat + i) % n_patch), device_id_type=MESH)

    n_plane = 2 * n_obs

    def plane(i):
        q = (obs * 2 + c + i) % n_plane
        return q // 2, z * 2 + q % 2

    @pl.loop(1, n_plane)
    def _(i):
        pl.semaphore_signal(barrier, inc=1, device_id=plane(i), device_id_type=MESH)

    nblk = rows // BAND

    @pl.loop(0, nblk)
    def _(i):
        r0 = pl.multiple_of(i * BAND, BAND)
        block = green[pl.ds(r0, BAND), :]
        hi, lo = split(block)
        ghi[pl.ds(r0, BAND), :] = hi
        glo[pl.ds(r0, BAND), :] = lo
        hi, lo = split(block.T)
        gthi[:, pl.ds(r0, BAND)] = hi
        gtlo[:, pl.ds(r0, BAND)] = lo
        hi, lo = split(data[pl.ds(r0, BAND), :])
        cat_r[pl.ds(r0, BAND), 0:E] = hi
        cat_r[pl.ds(r0, BAND), E:2 * E] = lo

    scs[...] = jnp.zeros((ITERS, 8, E), F32)
    zero_c = jnp.zeros((nc, R, E), F32)
    zero_h = jnp.zeros((BAND, E), F32)

    @pl.when(z == 0)
    def _():
        for it in range(ITERS):
            rl[it] = zero_c

    @pl.when(z == nz - 1)
    def _():
        for it in range(ITERS):
            rr[it] = zero_c

    @pl.when(pat == 0)
    def _():
        for it in range(ITERS):
            hal[it, 0] = zero_h
        for it in range(ITERS - 1):
            wr[it, 0] = zero_h

    @pl.when(pat == n_patch - 1)
    def _():
        for it in range(ITERS):
            hal[it, 1] = zero_h
        for it in range(ITERS - 1):
            wr[it, 1] = zero_h

    def build_laplace():
        @pl.loop(0, CB + 2)
        def _(j):
            r0 = pl.multiple_of(j * BAND, BAND)
            col = lax.broadcasted_iota(jnp.int32, (BAND, cols), 0) + j * BAND
            own = lax.broadcasted_iota(jnp.int32, (BAND, cols), 1) + BAND
            m = jnp.where(col == own, 4.0, 0.0)
            col = col + (pat * cols - BAND)
            for k in range(3):
                m = m - jnp.where(col == nb[k:k + 1, :], 1.0, 0.0)
            lmt[pl.ds(r0, BAND), :] = m.astype(BF16)
            lm[:, pl.ds(r0, BAND)] = m.T.astype(BF16)

    pl.semaphore_wait(barrier, n_patch - 1 + n_plane - 1)

    def bit_partner(p, j):
        b0, b1 = 1 << p, 1 << (nbit - 1 - p)
        bit = b0 + (j % 2) * (b1 - b0)
        return at(obs + bit * (1 - 2 * ((obs // bit) % 2)), pat)

    def bcopy(b, p, j):
        return rcopy(bb.at[b, p, j], br.at[b, p, j], pair(sem_b, b, p, j), bit_partner(p, j))

    def backward(b, hook, dst):
        for m in range(0, bc, per):
            y = dot(gthi[m * BR:(m + per) * BR, :], cat_r[...])
            y = y[:, :E] + y[:, E:] + dot(gtlo[m * BR:(m + per) * BR, :], cat_r[:, 0:E])
            bb[b, 0, m:m + per] = y.reshape(per, BR, E)
            for j in range(m, m + per):
                bcopy(b, 0, j).start()

        hook()
        for p in range(1, nbit):
            @pl.loop(0, bc)
            def _(j):
                bcopy(b, p - 1, j).wait_recv()
                bb[b, p, j] = bb[b, p - 1, j] + br[b, p - 1, j]
                bcopy(b, p, j).start()

        @pl.loop(0, bc)
        def _(j):
            bcopy(b, nbit - 1, j).wait_recv()
            dst[pl.ds(pl.multiple_of(j * BR, BR), BR), :] = bb[b, nbit - 1, j] + br[b, nbit - 1, j]

        for p in range(nbit):
            @pl.loop(0, bc)
            def _(j):
                bcopy(b, p, j).wait_send()

    def dcopy(it, k):
        return rcopy(pf.at[k], rd.at[it, k], pair(sem_d, it, k), at(obs, partner))

    def rcopy_up(it, src, k):
        return rcopy(src.at[k], rl.at[it, k], pair(sem_l, it, k), at(obs, pat + 2))

    def rcopy_down(it, src, k):
        return rcopy(src.at[k], rr.at[it, k], pair(sem_r, it, k), at(obs, pat - 2))

    def icopy(it, k):
        return rcopy(img.at[it, c, k], img.at[it, c, k], pair(sem_i, it, k), at(obs, partner))

    def put_cat(h, k, value):
        hi, lo = split(value)
        r0 = pl.multiple_of((h * nc + k) * R, R)
        cat_r[pl.ds(r0, R), 0:E] = hi
        cat_r[pl.ds(r0, R), E:2 * E] = lo

    def hcopy_r(it):
        return rcopy((a if it else g).at[pl.ds(cols - BAND, BAND)], hal.at[it, 0], pair(sem_h, it, 0), at(obs, pat + 1))

    def hcopy_l(it):
        return rcopy((a if it else g).at[pl.ds(0, BAND)], hal.at[it, 1], pair(sem_h, it, 1), at(obs, pat - 1))

    def forward(it, sums, hook):
        last = it == ITERS - 1

        @pl.when(has_r)
        def _():
            hcopy_r(it).start()

        @pl.when(has_l)
        def _():
            hcopy_l(it).start()

        hi, lo = split((a if it else g)[...])
        cat_d[:, 0:E] = hi
        cat_d[:, E:2 * E] = lo
        sums()

        def part(h):
            r0 = pl.multiple_of(h * half, half)
            y = dot(ghi[pl.ds(r0, half), :], cat_d[...])
            y = y[:, :E] + y[:, E:] + dot(glo[pl.ds(r0, half), :], cat_d[:, 0:E])
            return y.reshape(nc, R, E)

        pf[...] = part(other)

        @pl.loop(0, nc)
        def _(k):
            dcopy(it, k).start()

        s[...] = part(c)

        @pl.loop(0, nc)
        def _(k):
            dcopy(it, k).wait_recv()
            s[k] += rd[it, k]

            @pl.when(z == 0)
            def _():
                rcopy_up(it, s, k).start()

            @pl.when(z == nz - 1)
            def _():
                rcopy_down(it, s, k).start()

        def chain(t, ends=True):
            kl = t - lag * z
            kr = t - lag * (nz - 1 - z)
            kt = t - lag * jnp.maximum(z, nz - 1 - z)

            @pl.when(down & (kl >= 0) & (kl < nc))
            def _():
                rcopy_up(it, sr, kl).wait_recv()

                @pl.when(up)
                def _():
                    sr[kl] = rl[it, kl] + s[kl]
                    rcopy_up(it, sr, kl).start()

            @pl.when(up & (kr >= 0) & (kr < nc))
            def _():
                rcopy_down(it, sl, kr).wait_recv()

                @pl.when(down)
                def _():
                    sl[kr] = rr[it, kr] + s[kr]
                    rcopy_down(it, sl, kr).start()

            if not ends:
                return

            @pl.when((kt >= 0) & (kt < nc))
            def _():
                total = rl[it, kt] + s[kt] + rr[it, kt]
                if it:
                    step, ratio = scalars
                    rest = qg[kt] - step * total
                    total = rest + ratio * qd[kt]
                if not last:
                    qg[kt] = rest if it else total
                    qd[kt] = total
                if last:
                    sq[...] += jnp.sum((total * total).reshape(R // 8, 8, E), axis=0)
                else:
                    img[it, c, kt] = total
                    icopy(it, kt).start()
                    put_cat(c, kt, total)

        if last:
            sq[...] = jnp.zeros((8, E), F32)
        pl.loop(lag, lag * (nz // 2))(functools.partial(chain, ends=False))
        scalars = hook()
        pl.loop(lag * (nz // 2), nc + lag * (nz - 1))(chain)

        if not last:
            @pl.loop(0, nc)
            def _(k):
                icopy(it, k).wait_recv()
                put_cat(other, k, img[it, other, k])

        @pl.loop(0, nc)
        def _(k):
            dcopy(it, k).wait_send()
            if not last:
                icopy(it, k).wait_send()

            @pl.when(up)
            def _():
                rcopy_up(it, sr, k).wait_send()

            @pl.when(down)
            def _():
                rcopy_down(it, sl, k).wait_send()

    def halo_wait(it):
        @pl.when(has_l)
        def _():
            hcopy_r(it).wait_recv()

        @pl.when(has_r)
        def _():
            hcopy_l(it).wait_recv()

        @pl.when(has_r)
        def _():
            hcopy_r(it).wait_send()

        @pl.when(has_l)
        def _():
            hcopy_l(it).wait_send()

    def laplace():
        for r0, n, v in ((0, BAND, hd[0]), (BAND, cols, d[...]), (BAND + cols, BAND, hd[1])):
            hi, lo = split(v)
            cat_e[r0:r0 + n, 0:E] = hi
            cat_e[r0:r0 + n, E:2 * E] = lo

    def lap_rows(i):
        r0 = pl.multiple_of(i * BAND, BAND)
        y = dot(lm[pl.ds(r0, BAND), :], cat_e[...])
        return r0, weight * (y[:, :E] + y[:, E:])

    def wcopy_l(it):
        return rcopy(wext.at[pl.ds(0, BAND)], wr.at[it, 1], pair(sem_w, it, 1), at(obs, pat - 1))

    def wcopy_r(it):
        return rcopy(wext.at[pl.ds(BAND + cols, BAND)], wr.at[it, 0], pair(sem_w, it, 0), at(obs, pat + 1))

    def reg_start(it):
        laplace()

        @pl.loop(0, CB)
        def _(i):
            r0, u = lap_rows(i)
            hi, lo = split(u)
            cat_d[pl.ds(r0, BAND), 0:E] = hi
            cat_d[pl.ds(r0, BAND), E:2 * E] = lo

        @pl.loop(0, CB + 2)
        def _(i):
            r0 = pl.multiple_of(i * BAND, BAND)
            y = dot(lmt[pl.ds(r0, BAND), :], cat_d[...])
            wext[pl.ds(r0, BAND), :] = weight * (y[:, :E] + y[:, E:])

        @pl.when(has_l)
        def _():
            wcopy_l(it).start()

        @pl.when(has_r)
        def _():
            wcopy_r(it).start()

    def reg_end(it):
        a[...] += wext[BAND:BAND + cols, :]

        @pl.when(has_l)
        def _():
            wcopy_r(it).wait_recv()

        @pl.when(has_r)
        def _():
            wcopy_l(it).wait_recv()

        a[0:BAND, :] += wr[it, 0]
        a[cols - BAND:cols, :] += wr[it, 1]

        @pl.when(has_l)
        def _():
            wcopy_l(it).wait_send()

        @pl.when(has_r)
        def _():
            wcopy_r(it).wait_send()

    def scopy(it, slot, q):
        return rcopy(scs.at[it], scr.at[it, slot], (sem_s.at[0, it, q], sem_s.at[1, it, slot]), at(obs, q))

    def sums_start(it):
        scr[it, pat] = scs[it]

        @pl.loop(1, n_patch)
        def _(i):
            scopy(it, pat, (pat + i) % n_patch).start()

    def sums_end(it):
        @pl.loop(1, n_patch)
        def _(i):
            q = (pat + i) % n_patch
            scopy(it, q, q).wait_recv()

        @pl.loop(1, n_patch)
        def _(i):
            q = (pat + i) % n_patch
            scopy(it, pat, q).wait_send()

        return jnp.sum(scr[it], axis=0)

    def pcopy(slot, i):
        o, q = plane(i)
        return rcopy(pls, plr.at[slot], (sem_p.at[i], sem_n.at[slot]), (o, q))

    def rowsum(x):
        return jnp.sum(x, axis=0, keepdims=True)

    norms = []

    def dots(it):
        gv, dv, av = g[...], d[...], a[...]
        scs[it, 0:1, :] = rowsum(gv * gv)
        scs[it, 1:2, :] = rowsum(dv * av)
        scs[it, 2:3, :] = rowsum(gv * av)
        scs[it, 3:4, :] = rowsum(av * av)
        sums_start(it)

    def first():
        halo_wait(0)
        hg[...] = hal[0]
        hd[...] = hal[0]

    def advance(it):
        tot = sums_end(it - 1)
        if it == 1:
            norms.append(tot[0:1])
        norm = norms[-1]
        step = norm / tot[1:2]
        after = norm - 2.0 * step * tot[2:3] + step * step * tot[3:4]
        ratio = after / norm
        norms.append(after)
        halo_wait(it)
        if it == 1:
            slip[...] = step * d[...]
        else:
            slip[...] += step * d[...]
        g[...] = g[...] - step * a[...]
        d[...] = g[...] + ratio * d[...]
        hg[...] = hg[...] - step * hal[it]
        hd[...] = hg[...] + ratio * hd[...]
        if it == ITERS - 1:
            laplace()

            @pl.loop(0, CB)
            def _(i):
                _, u = lap_rows(i)
                scs[it] += jnp.sum((u * u).reshape(BAND // 8, 8, E), axis=0)

            sums_start(it)
        return step, ratio

    backward(0, build_laplace, g)
    d[...] = g[...]
    forward(0, lambda: None, first)
    for it in range(1, ITERS):
        backward(it, functools.partial(reg_start, it - 1), a)
        reg_end(it - 1)
        forward(it, functools.partial(dots, it - 1), functools.partial(advance, it))
    last = ITERS - 1
    norm = norms[-1]
    me = obs * 2 + c
    pls[...] = sq[...]
    plr[me] = sq[...]

    @pl.loop(1, n_plane)
    def _(i):
        pcopy(me, i).start()

    reg = rowsum(sums_end(last))

    @pl.loop(1, n_plane)
    def _(i):
        pcopy((me + i) % n_plane, i).wait_recv()

    curvature = rowsum(jnp.sum(plr[...], axis=0)) + reg
    out[...] = slip[...] + (norm / curvature) * d[...]

    @pl.loop(1, n_plane)
    def _(i):
        pcopy(me, i).wait_send()


def shards(green, data, neighbours, reg_weight):
    rows, cols = green.shape
    E = data.shape[1]
    n_obs, n_patch = lax.axis_size("obs"), lax.axis_size("patch")
    nbit = n_obs.bit_length() - 1
    nc = rows // 2 // 64
    bc = 8
    R, BR, ext = rows // 2 // nc, cols // bc, cols + 2 * BAND
    V = pltpu.VMEM
    D = pltpu.SemaphoreType.DMA
    scratch = [
        V((rows, cols), BF16), V((rows, cols), BF16),
        V((cols, rows), BF16), V((cols, rows), BF16),
        V((cols, ext), BF16), V((ext, cols), BF16),
        V((cols, 2 * E), BF16), V((rows, 2 * E), BF16), V((ext, 2 * E), BF16),
        V((cols, E), F32), V((cols, E), F32), V((cols, E), F32), V((ext, E), F32), V((cols, E), F32),
        V((8, E), F32),
        V((2, BAND, E), F32), V((2, BAND, E), F32), V((nc, R, E), F32), V((nc, R, E), F32),
        V((nc, R, E), F32), V((nc, R, E), F32), V((ITERS, nc, R, E), F32),
        V((nc, R, E), F32), V((nc, R, E), F32),
        V((ITERS, nc, R, E), F32), V((ITERS, nc, R, E), F32),
        V((ITERS - 1, 2, nc, R, E), F32),
        V((ITERS, nbit, bc, BR, E), F32), V((ITERS, nbit, bc, BR, E), F32),
        V((ITERS, 2, BAND, E), F32), V((ITERS - 1, 2, BAND, E), F32),
        V((ITERS, 8, E), F32), V((ITERS, n_patch, 8, E), F32),
        V((8, E), F32), V((2 * n_obs, 8, E), F32),
        D((2, ITERS, nc)), D((2, ITERS, nc)), D((2, ITERS, nc)), D((2, ITERS - 1, nc)),
        D((2, ITERS, nbit, bc)), D((2, ITERS, 2)), D((2, ITERS - 1, 2)),
        D((2, ITERS, n_patch)), D((2 * n_obs,)), D((2 * n_obs,)),
    ]
    return pl.pallas_call(
        functools.partial(kernel, n_obs, n_patch, nc, bc),
        out_shape=jax.ShapeDtypeStruct((cols, E), F32),
        in_specs=[pl.BlockSpec(memory_space=pltpu.VMEM)] * 4,
        out_specs=pl.BlockSpec(memory_space=pltpu.VMEM),
        scratch_shapes=scratch,
        compiler_params=pltpu.CompilerParams(
            collective_id=0, has_side_effects=True, vmem_limit_bytes=56 * 1024 * 1024),
    )(green, data, neighbours, reg_weight.reshape(1, E))


def solution(mesh):
    in_specs = (P("obs", "patch"), P("obs", None), P(None, "patch"), P())
    return jax.shard_map(shards, mesh=mesh, in_specs=in_specs, out_specs=P("patch", None), check_vma=False)
```

profile of v0, /device:TPU:0, one launch (start us, length us, event | category | flops | bytes accessed | tf_op | source)
XLA Modules:
  0.0 102.8 jit_solution(14333820264376346066)
XLA Ops:
  0.0 101.1 %shard_map.46 = f32[640,128]{1,0:T(8,128)} custom-call(f32[1280,640]{1,0:T(8,128)} %green.1, f32[1280,128]{1,0:T(8,128)} %data.1, s32[3,640]{1,0:T(4,128)} %nb.1, f32[1,128]{1,0:T(1,128)} %bitcast.1), custom_call_target="tpu_custom_call" | custom-call | tf_op jit(solution)/shard_map/pallas_call | solution.py:523
  101.1 1.7 %copy.6 = f32[640,128]{1,0:T(8,128)} copy(f32[640,128]{1,0:T(8,128)} %shard_map.46) | data formatting | bytes 655360
where the time goes:
time: 103 us
  Pallas kernels  101 us (98%)
  local copies, waits for them, and re-layouts  1.72 us (2%)
    pallas_call x1, Pallas kernels, shards(): pl.pallas_call(functools.partial(kernel, n_obs, n_patch, nc, bc), out_sha...  101 us

commit v1 on v0

v1 whole, which is shorter than its diff:
```python
import functools

import jax
import jax.numpy as jnp
from jax import lax
from jax.experimental import pallas as pl
from jax.experimental.pallas import tpu as pltpu
from jax.sharding import PartitionSpec as P

BAND = 128
ITERS = 3
MESH = pl.DeviceIdType.MESH
F32 = jnp.float32
BF16 = jnp.bfloat16
R = 64
LAG = 6


def dot(a, b):
    return lax.dot_general(a, b, (((1,), (0,)), ((), ())), preferred_element_type=F32)


def split(x):
    hi = x.astype(BF16)
    return hi, (x - hi.astype(F32)).astype(BF16)


def rowsum(x):
    return jnp.sum(x, axis=0, keepdims=True)


def kernel(n_obs, n_patch, nc, bc, green, data, nb, rw, out,
           gbuf, gpar, dbuf, ghi, glo, nbp, nbe, lm, lmt,
           cat_d, cat_e, cat_u, lt, lt0,
           d, g, a, wown, wsrc, slip, slp, dp, sq, hsrc, hd, hg, qd, qg,
           s, sr, sl, rl, rr, bb, br, nat, natp, hal, wr, scs, scr, pls, plr, tsrc, tdst,
           sem_l, sem_r, sem_b, sem_h, sem_w, sem_s, sem_p, sem_n, sem_x, sem_y, sem_g, sem_nb, sem_in):
    rows, cols = gbuf.shape
    E = dbuf.shape[1]
    H = E // 2
    CB = cols // BAND
    NB = 2 * CB
    RB = rows // (2 * BAND)
    nblk = rows // BAND
    per = BAND // R
    nz = n_patch // 2
    nbit = n_obs.bit_length() - 1
    obs = lax.axis_index("obs")
    pat = lax.axis_index("patch")
    z = pat // 2
    c = pat % 2
    other = 1 - c
    partner = z * 2 + other
    has_l, has_r = z > 0, z < nz - 1
    up, down = has_r, has_l
    n_plane = 2 * n_obs

    def lanes(n):
        return lax.broadcasted_iota(jnp.int32, (n, E), 1)

    def low(n):
        return lanes(n) < H

    def mine(n):
        i = lanes(n) - c * H
        return (i >= 0) & (i < H)

    def roll(x):
        return pltpu.roll(x, H, 1)

    def both(x):
        q = roll(x)
        m = low(x.shape[0])
        return jnp.where(m, x, q), jnp.where(m, q, x)

    def fold(x):
        return x + roll(x)

    def put_cat(ref, r0, v, third=False):
        n = v.shape[0]
        hi = v.astype(BF16)
        hf = hi.astype(F32)
        lf = v - hf
        m = low(n)
        ref[pl.ds(r0, n), 0:E] = jnp.where(m, hf, lf).astype(BF16)
        ref[pl.ds(r0, n), E:2 * E] = jnp.where(m, lf, hf).astype(BF16)
        if third:
            ref[pl.ds(r0, n), 2 * E:3 * E] = hi

    def rcopy(src, dst, sems, dev):
        return pltpu.make_async_remote_copy(
            src_ref=src, dst_ref=dst, send_sem=sems[0], recv_sem=sems[1],
            device_id=dev, device_id_type=MESH)

    def pair(sem, *idx):
        return sem.at[(0,) + idx], sem.at[(1,) + idx]

    def at(o, q):
        return (o, q)

    def plane(i):
        q = (obs * 2 + c + i) % n_plane
        return q // 2, z * 2 + q % 2

    def zpeer(i):
        return (z + i) % nz

    def load(i):
        r0 = pl.multiple_of(i * BAND, BAND)
        return pltpu.make_async_copy(green.at[pl.ds(r0, BAND)], gbuf.at[pl.ds(r0, BAND)], sem_in.at[i])

    load_data = pltpu.make_async_copy(data, dbuf, sem_in.at[nblk])
    load_data.start()

    @pl.loop(0, nblk)
    def _(i):
        load(i).start()

    barrier = pltpu.get_barrier_semaphore()

    @pl.loop(1, nz)
    def _(i):
        pl.semaphore_signal(barrier, inc=1, device_id=at(obs, zpeer(i) * 2 + c), device_id_type=MESH)

    @pl.loop(1, n_plane)
    def _(i):
        pl.semaphore_signal(barrier, inc=1, device_id=plane(i), device_id_type=MESH)

    wrow = rw[...]
    weight = jnp.where(mine(1), wrow, roll(wrow))

    scs[...] = jnp.zeros((ITERS, 8, E), F32)
    zero_c = jnp.zeros((nc, R, E), F32)
    zero_h = jnp.zeros((R, E), F32)
    zero_u = jnp.zeros((2 * BAND, 2 * E), BF16)
    cat_u[0:2 * BAND, :] = zero_u
    cat_u[(NB + 2) * BAND:(NB + 4) * BAND, :] = zero_u
    nbe[...] = jnp.full(nbe.shape, -(2 ** 24), jnp.int32)

    @pl.when(z == 0)
    def _():
        for it in range(ITERS):
            rl[it] = zero_c
            hal[it, 0] = zero_h
        for it in range(ITERS - 1):
            wr[it, 0] = zero_h

    @pl.when(z == nz - 1)
    def _():
        for it in range(ITERS):
            rr[it] = zero_c
            hal[it, 1] = zero_h
        for it in range(ITERS - 1):
            wr[it, 1] = zero_h

    load_data.wait()

    @pl.loop(0, nblk)
    def _(i):
        r0 = pl.multiple_of(i * BAND, BAND)
        hi, lo = split(dbuf[pl.ds(r0, BAND), :].T)
        lt0[0:E, pl.ds(r0, BAND)] = hi
        lt0[E:2 * E, pl.ds(r0, BAND)] = lo

    def put_green(src, i, core):
        r0 = pl.multiple_of(i * BAND, BAND)
        hi, lo = split(src[pl.ds(r0, BAND), :])
        for j in range(CB):
            c0 = pl.multiple_of((2 * j + core) * BAND, BAND)
            ghi[pl.ds(r0, BAND), pl.ds(c0, BAND)] = hi[:, j * BAND:(j + 1) * BAND]
            glo[pl.ds(r0, BAND), pl.ds(c0, BAND)] = lo[:, j * BAND:(j + 1) * BAND]

    @pl.loop(0, nblk)
    def _(i):
        load(i).wait()
        put_green(gbuf, i, c)

    pl.semaphore_wait(barrier, nz - 1 + n_plane - 1)

    ncopy = rcopy(nb, nbp, pair(sem_nb), at(obs, partner))
    ncopy.start()

    def gcopy(i):
        r0 = pl.multiple_of(i * BAND, BAND)
        return rcopy(gbuf.at[pl.ds(r0, BAND)], gpar.at[pl.ds(r0, BAND)], pair(sem_g, i), at(obs, partner))

    def build_laplace():
        ncopy.wait_recv()
        base = z * (2 * cols)
        own0 = pl.multiple_of((2 + c * CB) * BAND, BAND)
        par0 = pl.multiple_of((2 + other * CB) * BAND, BAND)
        nbe[0:3, pl.ds(own0, cols)] = nb[...] - base
        nbe[0:3, pl.ds(par0, cols)] = nbp[...] - base
        K = 3 * BAND

        @pl.loop(0, NB + 2)
        def _(j):
            r0 = pl.multiple_of(j * BAND, BAND)
            col = lax.broadcasted_iota(jnp.int32, (BAND, K), 0) + (j - 1) * BAND
            own = lax.broadcasted_iota(jnp.int32, (BAND, K), 1) + (j - 2) * BAND
            m = jnp.where(col == own, 4.0, 0.0)
            for k in range(3):
                m = m - jnp.where(col == nbe[k:k + 1, pl.ds(r0, K)], 1.0, 0.0)
            lmt[pl.ds(r0, BAND), :] = m.astype(BF16)

        @pl.loop(0, NB)
        def _(b):
            r0 = pl.multiple_of(b * BAND, BAND)
            n0 = pl.multiple_of((b + 2) * BAND, BAND)
            row = lax.broadcasted_iota(jnp.int32, (BAND, K), 0) + b * BAND
            col = lax.broadcasted_iota(jnp.int32, (BAND, K), 1) + (b - 1) * BAND
            m = jnp.where(col == row, 4.0, 0.0)
            t = nbe[0:8, pl.ds(n0, BAND)].T
            for k in range(3):
                m = m - jnp.where(col == t[:, k:k + 1], 1.0, 0.0)
            lm[pl.ds(r0, BAND), :] = m.astype(BF16)

    def bit_partner(p, j):
        b0, b1 = 1 << p, 1 << (nbit - 1 - p)
        bit = b0 + (j % 2) * (b1 - b0)
        return at(obs + bit * (1 - 2 * ((obs // bit) % 2)), pat)

    def bcopy(b, p, j):
        return rcopy(bb.at[b, p, j], br.at[b, p, j], pair(sem_b, b, p, j), bit_partner(p, j))

    def product(b, m):
        if b == 0:
            c0 = pl.multiple_of((2 * m + c) * BAND, BAND)
            y = dot(lt0[...], ghi[:, pl.ds(c0, BAND)])
            y = y[:E] + y[E:] + dot(lt0[0:E, :], glo[:, pl.ds(c0, BAND)])
            return y.T
        c0 = pl.multiple_of(m * 2 * BAND, 2 * BAND)
        y = dot(lt[...], ghi[:, pl.ds(c0, 2 * BAND)])
        y = y[:H] + y[H:] + dot(lt[0:H, :], glo[:, pl.ds(c0, 2 * BAND)])
        return jnp.concatenate([y[:, :BAND], y[:, BAND:]], axis=0).T

    def backward(b, hook, late, finish):
        @pl.loop(0, CB)
        def _(m):
            bb[b, 0, pl.ds(m * per, per)] = product(b, m).reshape(per, R, E)
            for k in range(per):
                bcopy(b, 0, m * per + k).start()

        hook()
        for p in range(1, nbit):
            @pl.loop(0, bc)
            def _(j):
                bcopy(b, p - 1, j).wait_recv()
                bb[b, p, j] = bb[b, p - 1, j] + br[b, p - 1, j]
                bcopy(b, p, j).start()

        late()

        @pl.loop(0, bc)
        def _(j):
            bcopy(b, nbit - 1, j).wait_recv()
            finish(j, bb[b, nbit - 1, j] + br[b, nbit - 1, j])

    def backward_sent(b):
        for p in range(nbit):
            @pl.loop(0, bc)
            def _(j):
                bcopy(b, p, j).wait_send()

    def rcopy_up(it, src, k):
        return rcopy(src.at[k], rl.at[it, k], pair(sem_l, it, k), at(obs, pat + 2))

    def rcopy_down(it, src, k):
        return rcopy(src.at[k], rr.at[it, k], pair(sem_r, it, k), at(obs, pat - 2))

    def hcopy_r(it):
        return rcopy(hsrc.at[it, 0], hal.at[it, 0], pair(sem_h, it, 0), at(obs, pat + 2))

    def hcopy_l(it):
        return rcopy(hsrc.at[it, 1], hal.at[it, 1], pair(sem_h, it, 1), at(obs, pat - 2))

    def put_lt(m):
        x = qd[pl.ds(m * per, per)].reshape(BAND, E)
        hi, lo = split(x.T)
        o0 = pl.multiple_of(m * 2 * BAND, 2 * BAND)
        o1 = pl.multiple_of(m * 2 * BAND + BAND, BAND)
        lt[0:H, pl.ds(o0, BAND)] = hi[:H]
        lt[H:E, pl.ds(o0, BAND)] = lo[:H]
        lt[0:H, pl.ds(o1, BAND)] = hi[H:]
        lt[H:E, pl.ds(o1, BAND)] = lo[H:]

    def forward(it, sums, hook):
        last = it == ITERS - 1
        v = a if it else g
        x = v[cols - BAND:cols, :]
        hsrc[it, 0] = jnp.where(low(R), roll(x[:R]), x[R:])
        x = v[0:BAND, :]
        hsrc[it, 1] = jnp.where(low(R), x[:R], roll(x[R:]))

        @pl.when(up & down)
        def _():
            hcopy_r(it).start()
            hcopy_l(it).start()

        @pl.loop(0, CB)
        def _(i):
            top, bot = both(v[pl.ds(pl.multiple_of(i * BAND, BAND), BAND), :])
            r0 = pl.multiple_of(i * 2 * BAND, 2 * BAND)
            put_cat(cat_d, r0, top, True)
            put_cat(cat_d, pl.multiple_of(r0 + BAND, BAND), bot, True)

        def group(m):
            r0 = pl.multiple_of(m * 2 * BAND, 2 * BAND)
            y = dot(ghi[pl.ds(r0, 2 * BAND), :], cat_d[:, 0:2 * E])
            y = y[:, :E] + y[:, E:] + dot(glo[pl.ds(r0, 2 * BAND), :], cat_d[:, 2 * E:3 * E])
            y = jnp.where(low(BAND), y[:BAND], y[BAND:])
            s[pl.ds(m * per, per)] = y.reshape(per, R, E)
            for k in range(per):
                @pl.when(z == 0)
                def _():
                    rcopy_up(it, s, m * per + k).start()

                @pl.when(z == nz - 1)
                def _():
                    rcopy_down(it, s, m * per + k).start()

        group(0)
        sums()

        @pl.when(up & (z == 0))
        def _():
            hcopy_r(it).start()

        @pl.when(down & (z == nz - 1))
        def _():
            hcopy_l(it).start()

        pl.loop(1, RB)(group)
        backward_sent(it)

        def chain(t, ends=True):
            kl = t - LAG * z
            kr = t - LAG * (nz - 1 - z)
            kt = t - LAG * jnp.maximum(z, nz - 1 - z)

            @pl.when(down & (kl >= 0) & (kl < nc))
            def _():
                rcopy_up(it, sr, kl).wait_recv()

                @pl.when(up)
                def _():
                    sr[kl] = rl[it, kl] + s[kl]
                    rcopy_up(it, sr, kl).start()

            @pl.when(up & (kr >= 0) & (kr < nc))
            def _():
                rcopy_down(it, sl, kr).wait_recv()

                @pl.when(down)
                def _():
                    sl[kr] = rr[it, kr] + s[kr]
                    rcopy_down(it, sl, kr).start()

            if not ends:
                return

            @pl.when((kt >= 0) & (kt < nc))
            def _():
                total = rl[it, kt] + s[kt] + rr[it, kt]
                if it:
                    step, ratio = scalars
                    rest = qg[kt] - step * total
                    total = rest + ratio * qd[kt]
                if last:
                    sq[...] += jnp.sum((total * total).reshape(R // 8, 8, E), axis=0)
                else:
                    qg[kt] = rest if it else total
                    qd[kt] = total

                    @pl.when(kt % per == per - 1)
                    def _():
                        put_lt(kt // per)

        if last:
            sq[...] = jnp.zeros((8, E), F32)
        pl.loop(LAG, LAG * (nz // 2))(functools.partial(chain, ends=False))
        scalars = hook()
        pl.loop(LAG * (nz // 2), nc + LAG * (nz - 1))(chain)

    def forward_sent(it):
        @pl.loop(0, nc)
        def _(k):
            @pl.when(up)
            def _():
                rcopy_up(it, sr, k).wait_send()

            @pl.when(down)
            def _():
                rcopy_down(it, sl, k).wait_send()

        @pl.when(up)
        def _():
            hcopy_r(it).wait_send()

        @pl.when(down)
        def _():
            hcopy_l(it).wait_send()

    def halo_wait(it):
        @pl.when(has_l)
        def _():
            hcopy_r(it).wait_recv()

        @pl.when(has_r)
        def _():
            hcopy_l(it).wait_recv()

    def widen(x):
        top, bot = both(x)
        return jnp.concatenate([top, bot], axis=0)

    def laplace():
        put_cat(cat_e, 0, widen(hd[0]))
        put_cat(cat_e, (NB + 1) * BAND, widen(hd[1]))

        @pl.loop(0, CB)
        def _(i):
            top, bot = both(d[pl.ds(pl.multiple_of(i * BAND, BAND), BAND), :])
            put_cat(cat_e, pl.multiple_of((i + 1) * BAND, BAND), top)
            put_cat(cat_e, pl.multiple_of((CB + i + 1) * BAND, BAND), bot)

    def banded(mat, vec, j):
        r0 = pl.multiple_of(j * BAND, BAND)
        y = dot(mat[pl.ds(r0, BAND), :], vec[pl.ds(r0, 3 * BAND), :])
        return y[:, :E] + y[:, E:]

    def lap_rows(i):
        return weight * jnp.where(low(BAND), banded(lm, cat_e, i), banded(lm, cat_e, CB + i))

    def wcopy_l(it):
        return rcopy(wsrc.at[it, 0], wr.at[it, 1], pair(sem_w, it, 1), at(obs, pat - 2))

    def wcopy_r(it):
        return rcopy(wsrc.at[it, 1], wr.at[it, 0], pair(sem_w, it, 0), at(obs, pat + 2))

    def reg_start(it):
        laplace()

        @pl.loop(0, CB)
        def _(i):
            top, bot = both(lap_rows(i))
            put_cat(cat_u, pl.multiple_of((i + 2) * BAND, BAND), top)
            put_cat(cat_u, pl.multiple_of((CB + i + 2) * BAND, BAND), bot)

        for side, j in ((0, 0), (1, NB + 1)):
            y = banded(lmt, cat_u, j)
            wsrc[it, side] = weight * jnp.where(low(R), y[:R], y[R:])

        @pl.when(has_l)
        def _():
            wcopy_l(it).start()

        @pl.when(has_r)
        def _():
            wcopy_r(it).start()

    def reg_own():
        @pl.loop(0, CB)
        def _(i):
            y = jnp.where(low(BAND), banded(lmt, cat_u, i + 1), banded(lmt, cat_u, CB + i + 1))
            wown[pl.ds(pl.multiple_of(i * BAND, BAND), BAND), :] = weight * y

    def reg_end(it):
        @pl.when(has_l)
        def _():
            wcopy_r(it).wait_recv()

        @pl.when(has_r)
        def _():
            wcopy_l(it).wait_recv()

        a[0:BAND, :] += jnp.where(low(BAND), widen(wr[it, 0]), 0.0)
        a[cols - BAND:cols, :] += jnp.where(low(BAND), 0.0, widen(wr[it, 1]))

    def reg_sent(it):
        @pl.when(has_l)
        def _():
            wcopy_l(it).wait_send()

        @pl.when(has_r)
        def _():
            wcopy_r(it).wait_send()

    def scopy(it, slot, q):
        return rcopy(scs.at[it], scr.at[it, slot], (sem_s.at[0, it, q], sem_s.at[1, it, slot]), at(obs, q * 2 + c))

    def sums_start(it):
        scr[it, z] = scs[it]

        @pl.loop(1, nz)
        def _(i):
            scopy(it, z, zpeer(i)).start()

    def sums_end(it):
        @pl.loop(1, nz)
        def _(i):
            scopy(it, zpeer(i), zpeer(i)).wait_recv()

        return fold(jnp.sum(scr[it], axis=0))

    def sums_sent(it):
        @pl.loop(1, nz)
        def _(i):
            scopy(it, z, zpeer(i)).wait_send()

    def pcopy(o, q, i):
        po, pp = plane(i)
        return rcopy(pls, plr.at[o, q], (sem_p.at[i], sem_n.at[o, q]), (po, pp))

    norms = []

    def dots(it):
        gv, dv, av = g[...], d[...], a[...]
        scs[it, 0:1, :] = rowsum(gv * gv)
        scs[it, 1:2, :] = rowsum(dv * av)
        scs[it, 2:3, :] = rowsum(gv * av)
        scs[it, 3:4, :] = rowsum(av * av)
        sums_start(it)

    def first():
        halo_wait(0)
        hg[...] = hal[0]
        hd[...] = hal[0]

    def ycopy(i):
        return rcopy((slip, d)[i], (slp, dp)[i], pair(sem_y, i), at(obs, partner))

    tcopy = rcopy(tsrc, tdst, pair(sem_y, 2), at(obs, partner))

    def advance(it):
        tot = sums_end(it - 1)
        if it == 1:
            norms.append(tot[0:1])
        norm = norms[-1]
        step = norm / tot[1:2]
        after = norm - 2.0 * step * tot[2:3] + step * step * tot[3:4]
        ratio = after / norm
        norms.append(after)
        halo_wait(it)
        if it == 1:
            slip[...] = step * d[...]
        else:
            slip[...] += step * d[...]
        g[...] = g[...] - step * a[...]
        d[...] = g[...] + ratio * d[...]
        hg[...] = hg[...] - step * hal[it]
        hd[...] = hg[...] + ratio * hd[...]
        if it == ITERS - 1:
            ycopy(0).start()
            ycopy(1).start()
            laplace()

            @pl.loop(0, CB)
            def _(i):
                u = lap_rows(i)
                scs[it] += jnp.sum((u * u).reshape(BAND // 8, 8, E), axis=0)

            sums_start(it)
        return step, ratio

    def xcopy(j):
        return rcopy(nat.at[j], natp.at[j], pair(sem_x, j), at(obs, partner))

    def first_hook():
        @pl.loop(0, nblk)
        def _(i):
            gcopy(i).start()

        build_laplace()

    def first_late():
        @pl.loop(0, nblk)
        def _(i):
            gcopy(i).wait_recv()
            put_green(gpar, i, other)

    def first_finish(j, x):
        nat[j] = x
        xcopy(j).start()

    backward(0, first_hook, first_late, first_finish)

    @pl.loop(0, bc)
    def _(j):
        xcopy(j).wait_recv()
        r0 = pl.multiple_of(j * R, R)
        x = jnp.where(mine(R), nat[j], roll(natp[j]))
        g[pl.ds(r0, R), :] = x
        d[pl.ds(r0, R), :] = x

    forward(0, lambda: None, first)
    for it in range(1, ITERS):
        def hook(it=it):
            forward_sent(it - 1)
            reg_start(it - 1)

        def finish(j, x):
            r0 = pl.multiple_of(j * R, R)
            a[pl.ds(r0, R), :] = x + wown[pl.ds(r0, R), :]

        backward(it, hook, reg_own, finish)
        reg_end(it - 1)
        forward(it, functools.partial(dots, it - 1), functools.partial(advance, it))

    last = ITERS - 1
    norm = norms[-1]
    pls[...] = sq[...]
    plr[obs, c] = sq[...]

    @pl.loop(1, n_plane)
    def _(i):
        pcopy(obs, c, i).start()

    @pl.loop(1, nz)
    def _(i):
        scopy(last, zpeer(i), zpeer(i)).wait_recv()

    tsrc[0:1, :] = norm
    tsrc[1:2, :] = fold(rowsum(jnp.sum(scr[last], axis=0)))
    tcopy.start()

    forward_sent(last)
    for it in range(ITERS):
        sums_sent(it)
    for it in range(ITERS - 1):
        reg_sent(it)
    ncopy.wait_send()

    @pl.loop(0, nblk)
    def _(i):
        gcopy(i).wait_send()

    @pl.loop(0, bc)
    def _(j):
        xcopy(j).wait_send()

    ycopy(0).wait_recv()
    ycopy(1).wait_recv()
    tcopy.wait_recv()

    @pl.loop(1, n_plane)
    def _(i):
        q = (obs * 2 + c + i) % n_plane
        pcopy(q // 2, q % 2, i).wait_recv()

    def step_of(t, q):
        return t[0:1, :] / (fold(rowsum(jnp.sum(plr[:, q], axis=0))) + t[1:2, :])

    step = jnp.where(mine(1), step_of(tsrc, c), step_of(tdst, other))

    @pl.loop(0, CB)
    def _(i):
        blk = pl.ds(pl.multiple_of(i * BAND, BAND), BAND)
        m = mine(BAND)
        out[blk, :] = jnp.where(m, slip[blk, :], roll(slp[blk, :])) + step * jnp.where(m, d[blk, :], roll(dp[blk, :]))

    ycopy(0).wait_send()
    ycopy(1).wait_send()
    tcopy.wait_send()

    @pl.loop(1, n_plane)
    def _(i):
        pcopy(obs, c, i).wait_send()


def shards(green, data, neighbours, reg_weight):
    rows, cols = green.shape
    E = data.shape[1]
    n_obs, n_patch = lax.axis_size("obs"), lax.axis_size("patch")
    nbit = n_obs.bit_length() - 1
    nz = n_patch // 2
    nc, bc = rows // 2 // R, cols // R
    NB = 2 * cols // BAND
    nblk = rows // BAND
    V = pltpu.VMEM
    D = pltpu.SemaphoreType.DMA
    scratch = [
        V((rows, cols), F32), V((rows, cols), F32), V((rows, E), F32),
        V((rows, 2 * cols), BF16), V((rows, 2 * cols), BF16),
        V(neighbours.shape, jnp.int32), V((8, (NB + 4) * BAND), jnp.int32),
        V((NB * BAND, 3 * BAND), BF16), V(((NB + 2) * BAND, 3 * BAND), BF16),
        V((2 * cols, 3 * E), BF16), V(((NB + 2) * BAND, 2 * E), BF16), V(((NB + 4) * BAND, 2 * E), BF16),
        V((E, rows), BF16), V((2 * E, rows), BF16),
        V((cols, E), F32), V((cols, E), F32), V((cols, E), F32), V((cols, E), F32), V((ITERS - 1, 2, R, E), F32),
        V((cols, E), F32), V((cols, E), F32), V((cols, E), F32), V((8, E), F32),
        V((ITERS, 2, R, E), F32), V((2, R, E), F32), V((2, R, E), F32), V((nc, R, E), F32), V((nc, R, E), F32),
        V((nc, R, E), F32), V((nc, R, E), F32), V((nc, R, E), F32),
        V((ITERS, nc, R, E), F32), V((ITERS, nc, R, E), F32),
        V((ITERS, nbit, bc, R, E), F32), V((ITERS, nbit, bc, R, E), F32),
        V((bc, R, E), F32), V((bc, R, E), F32),
        V((ITERS, 2, R, E), F32), V((ITERS - 1, 2, R, E), F32),
        V((ITERS, 8, E), F32), V((ITERS, nz, 8, E), F32),
        V((8, E), F32), V((n_obs, 2, 8, E), F32), V((8, E), F32), V((8, E), F32),
        D((2, ITERS, nc)), D((2, ITERS, nc)), D((2, ITERS, nbit, bc)), D((2, ITERS, 2)), D((2, ITERS - 1, 2)),
        D((2, ITERS, nz)), D((2 * n_obs,)), D((n_obs, 2)), D((2, bc)), D((2, 3)), D((2, nblk)), D((2,)),
        D((nblk + 1,)),
    ]
    return pl.pallas_call(
        functools.partial(kernel, n_obs, n_patch, nc, bc),
        out_shape=jax.ShapeDtypeStruct((cols, E), F32),
        in_specs=[pl.BlockSpec(memory_space=pl.ANY)] * 2 + [pl.BlockSpec(memory_space=pltpu.VMEM)] * 2,
        out_specs=pl.BlockSpec(memory_space=pltpu.VMEM),
        scratch_shapes=scratch,
        compiler_params=pltpu.CompilerParams(
            collective_id=0, has_side_effects=True, vmem_limit_bytes=56 * 1024 * 1024),
    )(green, data, neighbours, reg_weight.reshape(1, E))


def solution(mesh):
    in_specs = (P("obs", "patch"), P("obs", None), P(None, "patch"), P())
    return jax.shard_map(shards, mesh=mesh, in_specs=in_specs, out_specs=P("patch", None), check_vma=False)
```

time: 103 us -> 98.8 us (0.959)
  Pallas kernels: 101 us -> 96.9 us
    pallas_call x1, Pallas kernels: 101 us -> 96.9 us  [shards(): pl.pallas_call(functools.partial(kernel, n_obs, n_patch, nc, bc), out_sha...]
where the time goes in v1:
time: 98.8 us; the launch traced here: 98.6 us
  Pallas kernels  96.9 us (98%)
  local copies, waits for them, and re-layouts  1.72 us (2%)
    pallas_call x1, Pallas kernels, shards(): pl.pallas_call(functools.partial(kernel, n_obs, n_patch, nc, bc), out_sha...  96.9 us

profile of v1, /device:TPU:0, one launch (start us, length us, event | category | flops | bytes accessed | tf_op | source)
XLA Modules:
  0.0 98.6 jit_solution(8062291132087992549)
XLA Ops:
  0.0 96.9 %shard_map.46 = f32[640,128]{1,0:T(8,128)} custom-call(f32[1280,640]{1,0:T(8,128)} %green.1, f32[1280,128]{1,0:T(8,128)} %data.1, s32[3,640]{1,0:T(4,128)} %nb.1, f32[1,128]{1,0:T(1,128)} %bitcast.1), custom_call_target="tpu_custom_call" | custom-call | tf_op jit(solution)/shard_map/pallas_call | solution.py:703
  96.9 1.7 %copy.6 = f32[640,128]{1,0:T(8,128)} copy(f32[640,128]{1,0:T(8,128)} %shard_map.46) | data formatting | bytes 655360

commit v2 on v1

--- a/solution.py
+++ b/solution.py
@@ -53,6 +53,7 @@
     partner = z * 2 + other
     has_l, has_r = z > 0, z < nz - 1
     up, down = has_r, has_l
+    inner = up & down
     n_plane = 2 * n_obs
 
     def lanes(n):
@@ -129,38 +130,13 @@
     wrow = rw[...]
     weight = jnp.where(mine(1), wrow, roll(wrow))
 
-    scs[...] = jnp.zeros((ITERS, 8, E), F32)
-    zero_c = jnp.zeros((nc, R, E), F32)
-    zero_h = jnp.zeros((R, E), F32)
-    zero_u = jnp.zeros((2 * BAND, 2 * E), BF16)
-    cat_u[0:2 * BAND, :] = zero_u
-    cat_u[(NB + 2) * BAND:(NB + 4) * BAND, :] = zero_u
-    nbe[...] = jnp.full(nbe.shape, -(2 ** 24), jnp.int32)
-
-    @pl.when(z == 0)
-    def _():
-        for it in range(ITERS):
-            rl[it] = zero_c
-            hal[it, 0] = zero_h
-        for it in range(ITERS - 1):
-            wr[it, 0] = zero_h
-
-    @pl.when(z == nz - 1)
-    def _():
-        for it in range(ITERS):
-            rr[it] = zero_c
-            hal[it, 1] = zero_h
-        for it in range(ITERS - 1):
-            wr[it, 1] = zero_h
-
     load_data.wait()
 
-    @pl.loop(0, nblk)
-    def _(i):
-        r0 = pl.multiple_of(i * BAND, BAND)
-        hi, lo = split(dbuf[pl.ds(r0, BAND), :].T)
-        lt0[0:E, pl.ds(r0, BAND)] = hi
-        lt0[E:2 * E, pl.ds(r0, BAND)] = lo
+    for i in range(nblk):
+        r0 = i * BAND
+        hi, lo = split(dbuf[r0:r0 + BAND, :].T)
+        lt0[0:E, r0:r0 + BAND] = hi
+        lt0[E:2 * E, r0:r0 + BAND] = lo
 
     def put_green(src, i, core):
         r0 = pl.multiple_of(i * BAND, BAND)
@@ -186,6 +162,10 @@
 
     def build_laplace():
         ncopy.wait_recv()
+        zero_u = jnp.zeros((2 * BAND, 2 * E), BF16)
+        cat_u[0:2 * BAND, :] = zero_u
+        cat_u[(NB + 2) * BAND:(NB + 4) * BAND, :] = zero_u
+        nbe[...] = jnp.full(nbe.shape, -(2 ** 24), jnp.int32)
         base = z * (2 * cols)
         own0 = pl.multiple_of((2 + c * CB) * BAND, BAND)
         par0 = pl.multiple_of((2 + other * CB) * BAND, BAND)
@@ -193,9 +173,8 @@
         nbe[0:3, pl.ds(par0, cols)] = nbp[...] - base
         K = 3 * BAND
 
-        @pl.loop(0, NB + 2)
-        def _(j):
-            r0 = pl.multiple_of(j * BAND, BAND)
+        for j in range(NB + 2):
+            r0 = j * BAND
             col = lax.broadcasted_iota(jnp.int32, (BAND, K), 0) + (j - 1) * BAND
             own = lax.broadcasted_iota(jnp.int32, (BAND, K), 1) + (j - 2) * BAND
             m = jnp.where(col == own, 4.0, 0.0)
@@ -203,10 +182,8 @@
                 m = m - jnp.where(col == nbe[k:k + 1, pl.ds(r0, K)], 1.0, 0.0)
             lmt[pl.ds(r0, BAND), :] = m.astype(BF16)
 
-        @pl.loop(0, NB)
-        def _(b):
-            r0 = pl.multiple_of(b * BAND, BAND)
-            n0 = pl.multiple_of((b + 2) * BAND, BAND)
+        for b in range(NB):
+            r0, n0 = b * BAND, (b + 2) * BAND
             row = lax.broadcasted_iota(jnp.int32, (BAND, K), 0) + b * BAND
             col = lax.broadcasted_iota(jnp.int32, (BAND, K), 1) + (b - 1) * BAND
             m = jnp.where(col == row, 4.0, 0.0)
@@ -214,6 +191,27 @@
             for k in range(3):
                 m = m - jnp.where(col == t[:, k:k + 1], 1.0, 0.0)
             lm[pl.ds(r0, BAND), :] = m.astype(BF16)
+
+    def clear():
+        scs[...] = jnp.zeros((ITERS, 8, E), F32)
+        zero_c = jnp.zeros((nc, R, E), F32)
+        zero_h = jnp.zeros((R, E), F32)
+
+        @pl.when(z == 0)
+        def _():
+            for it in range(ITERS):
+                rl[it] = zero_c
+                hal[it, 0] = zero_h
+            for it in range(ITERS - 1):
+                wr[it, 0] = zero_h
+
+        @pl.when(z == nz - 1)
+        def _():
+            for it in range(ITERS):
+                rr[it] = zero_c
+                hal[it, 1] = zero_h
+            for it in range(ITERS - 1):
+                wr[it, 1] = zero_h
 
     def bit_partner(p, j):
         b0, b1 = 1 << p, 1 << (nbit - 1 - p)
@@ -235,9 +233,8 @@
         return jnp.concatenate([y[:, :BAND], y[:, BAND:]], axis=0).T
 
     def backward(b, hook, late, finish):
-        @pl.loop(0, CB)
-        def _(m):
-            bb[b, 0, pl.ds(m * per, per)] = product(b, m).reshape(per, R, E)
+        for m in range(CB):
+            bb[b, 0, m * per:(m + 1) * per] = product(b, m).reshape(per, R, E)
             for k in range(per):
                 bcopy(b, 0, m * per + k).start()
 
@@ -284,7 +281,7 @@
         lt[0:H, pl.ds(o1, BAND)] = hi[H:]
         lt[H:E, pl.ds(o1, BAND)] = lo[H:]
 
-    def forward(it, sums, hook):
+    def forward(it, sums, after, hook):
         last = it == ITERS - 1
         v = a if it else g
         x = v[cols - BAND:cols, :]
@@ -297,19 +294,12 @@
             hcopy_r(it).start()
             hcopy_l(it).start()
 
-        @pl.loop(0, CB)
-        def _(i):
-            top, bot = both(v[pl.ds(pl.multiple_of(i * BAND, BAND), BAND), :])
-            r0 = pl.multiple_of(i * 2 * BAND, 2 * BAND)
-            put_cat(cat_d, r0, top, True)
-            put_cat(cat_d, pl.multiple_of(r0 + BAND, BAND), bot, True)
-
         def group(m):
-            r0 = pl.multiple_of(m * 2 * BAND, 2 * BAND)
-            y = dot(ghi[pl.ds(r0, 2 * BAND), :], cat_d[:, 0:2 * E])
-            y = y[:, :E] + y[:, E:] + dot(glo[pl.ds(r0, 2 * BAND), :], cat_d[:, 2 * E:3 * E])
+            r0 = m * 2 * BAND
+            y = dot(ghi[r0:r0 + 2 * BAND, :], cat_d[:, 0:2 * E])
+            y = y[:, :E] + y[:, E:] + dot(glo[r0:r0 + 2 * BAND, :], cat_d[:, 2 * E:3 * E])
             y = jnp.where(low(BAND), y[:BAND], y[BAND:])
-            s[pl.ds(m * per, per)] = y.reshape(per, R, E)
+            s[m * per:(m + 1) * per] = y.reshape(per, R, E)
             for k in range(per):
                 @pl.when(z == 0)
                 def _():
@@ -330,7 +320,9 @@
         def _():
             hcopy_l(it).start()
 
-        pl.loop(1, RB)(group)
+        for m in range(1, RB):
+            group(m)
+        after()
         backward_sent(it)
 
         def chain(t, ends=True):
@@ -380,7 +372,16 @@
             sq[...] = jnp.zeros((8, E), F32)
         pl.loop(LAG, LAG * (nz // 2))(functools.partial(chain, ends=False))
         scalars = hook()
+
+        @pl.when(jnp.logical_not(inner))
+        def _():
+            reg_sums() if last else reg_work(it)
+
         pl.loop(LAG * (nz // 2), nc + LAG * (nz - 1))(chain)
+        if last:
+            @pl.when(inner)
+            def _():
+                reg_sums()
 
     def forward_sent(it):
         @pl.loop(0, nc)
@@ -418,15 +419,14 @@
         put_cat(cat_e, 0, widen(hd[0]))
         put_cat(cat_e, (NB + 1) * BAND, widen(hd[1]))
 
-        @pl.loop(0, CB)
-        def _(i):
-            top, bot = both(d[pl.ds(pl.multiple_of(i * BAND, BAND), BAND), :])
-            put_cat(cat_e, pl.multiple_of((i + 1) * BAND, BAND), top)
-            put_cat(cat_e, pl.multiple_of((CB + i + 1) * BAND, BAND), bot)
+        for i in range(CB):
+            top, bot = both(d[i * BAND:(i + 1) * BAND, :])
+            put_cat(cat_e, (i + 1) * BAND, top)
+            put_cat(cat_e, (CB + i + 1) * BAND, bot)
 
     def banded(mat, vec, j):
-        r0 = pl.multiple_of(j * BAND, BAND)
-        y = dot(mat[pl.ds(r0, BAND), :], vec[pl.ds(r0, 3 * BAND), :])
+        r0 = j * BAND
+        y = dot(mat[r0:r0 + BAND, :], vec[r0:r0 + 3 * BAND, :])
         return y[:, :E] + y[:, E:]
 
     def lap_rows(i):
@@ -438,14 +438,13 @@
     def wcopy_r(it):
         return rcopy(wsrc.at[it, 1], wr.at[it, 0], pair(sem_w, it, 0), at(obs, pat + 2))
 
-    def reg_start(it):
+    def reg_work(it):
         laplace()
 
-        @pl.loop(0, CB)
-        def _(i):
+        for i in range(CB):
             top, bot = both(lap_rows(i))
-            put_cat(cat_u, pl.multiple_of((i + 2) * BAND, BAND), top)
-            put_cat(cat_u, pl.multiple_of((CB + i + 2) * BAND, BAND), bot)
+            put_cat(cat_u, (i + 2) * BAND, top)
+            put_cat(cat_u, (CB + i + 2) * BAND, bot)
 
         for side, j in ((0, 0), (1, NB + 1)):
             y = banded(lmt, cat_u, j)
@@ -459,11 +458,17 @@
         def _():
             wcopy_r(it).start()
 
-    def reg_own():
-        @pl.loop(0, CB)
-        def _(i):
+        for i in range(CB):
             y = jnp.where(low(BAND), banded(lmt, cat_u, i + 1), banded(lmt, cat_u, CB + i + 1))
-            wown[pl.ds(pl.multiple_of(i * BAND, BAND), BAND), :] = weight * y
+            wown[i * BAND:(i + 1) * BAND, :] = weight * y
+
+    def reg_sums():
+        last = ITERS - 1
+        laplace()
+        for i in range(CB):
+            u = lap_rows(i)
+            scs[last] += jnp.sum((u * u).reshape(BAND // 8, 8, E), axis=0)
+        sums_start(last)
 
     def reg_end(it):
         @pl.when(has_l)
@@ -474,8 +479,8 @@
         def _():
             wcopy_l(it).wait_recv()
 
-        a[0:BAND, :] += jnp.where(low(BAND), widen(wr[it, 0]), 0.0)
-        a[cols - BAND:cols, :] += jnp.where(low(BAND), 0.0, widen(wr[it, 1]))
+        wown[0:BAND, :] += jnp.where(low(BAND), widen(wr[it, 0]), 0.0)
+        wown[cols - BAND:cols, :] += jnp.where(low(BAND), 0.0, widen(wr[it, 1]))
 
     def reg_sent(it):
         @pl.when(has_l)
@@ -553,14 +558,6 @@
         if it == ITERS - 1:
             ycopy(0).start()
             ycopy(1).start()
-            laplace()
-
-            @pl.loop(0, CB)
-            def _(i):
-                u = lap_rows(i)
-                scs[it] += jnp.sum((u * u).reshape(BAND // 8, 8, E), axis=0)
-
-            sums_start(it)
         return step, ratio
 
     def xcopy(j):
@@ -571,7 +568,7 @@
         def _(i):
             gcopy(i).start()
 
-        build_laplace()
+        clear()
 
     def first_late():
         @pl.loop(0, nblk)
@@ -582,6 +579,12 @@
     def first_finish(j, x):
         nat[j] = x
         xcopy(j).start()
+
+    def put_operand(ref, i):
+        top, bot = both(ref[pl.ds(pl.multiple_of(i * BAND, BAND), BAND), :])
+        r0 = pl.multiple_of(i * 2 * BAND, 2 * BAND)
+        put_cat(cat_d, r0, top, True)
+        put_cat(cat_d, pl.multiple_of(r0 + BAND, BAND), bot, True)
 
     backward(0, first_hook, first_late, first_finish)
 
@@ -593,19 +596,30 @@
         g[pl.ds(r0, R), :] = x
         d[pl.ds(r0, R), :] = x
 
-    forward(0, lambda: None, first)
+        @pl.when(j % per == per - 1)
+        def _():
+            put_operand(g, j // per)
+
+    pl.when(c == 0)(build_laplace)
+    forward(0, lambda: None, lambda: pl.when(c == 1)(build_laplace), first)
     for it in range(1, ITERS):
         def hook(it=it):
             forward_sent(it - 1)
-            reg_start(it - 1)
+
+            @pl.when(inner)
+            def _():
+                reg_work(it - 1)
 
         def finish(j, x):
             r0 = pl.multiple_of(j * R, R)
             a[pl.ds(r0, R), :] = x + wown[pl.ds(r0, R), :]
 
-        backward(it, hook, reg_own, finish)
-        reg_end(it - 1)
-        forward(it, functools.partial(dots, it - 1), functools.partial(advance, it))
+            @pl.when(j % per == per - 1)
+            def _():
+                put_operand(a, j // per)
+
+        backward(it, hook, functools.partial(reg_end, it - 1), finish)
+        forward(it, functools.partial(dots, it - 1), lambda: None, functools.partial(advance, it))
 
     last = ITERS - 1
     norm = norms[-1]
@@ -641,7 +655,15 @@
 
     ycopy(0).wait_recv()
     ycopy(1).wait_recv()
+    ycopy(0).wait_send()
+    ycopy(1).wait_send()
+    for i in range(CB):
+        blk = slice(i * BAND, (i + 1) * BAND)
+        m = mine(BAND)
+        slip[blk, :] = jnp.where(m, slip[blk, :], roll(slp[blk, :]))
+        d[blk, :] = jnp.where(m, d[blk, :], roll(dp[blk, :]))
     tcopy.wait_recv()
+    tcopy.wait_send()
 
     @pl.loop(1, n_plane)
     def _(i):
@@ -653,15 +675,7 @@
 
     step = jnp.where(mine(1), step_of(tsrc, c), step_of(tdst, other))
 
-    @pl.loop(0, CB)
-    def _(i):
-        blk = pl.ds(pl.multiple_of(i * BAND, BAND), BAND)
-        m = mine(BAND)
-        out[blk, :] = jnp.where(m, slip[blk, :], roll(slp[blk, :])) + step * jnp.where(m, d[blk, :], roll(dp[blk, :]))
-
-    ycopy(0).wait_send()
-    ycopy(1).wait_send()
-    tcopy.wait_send()
+    out[...] = slip[...] + step * d[...]
 
     @pl.loop(1, n_plane)
     def _(i):

time: 98.8 us -> 89.4 us (0.905)
  Pallas kernels: 96.9 us -> 87.5 us
    pallas_call x1, Pallas kernels: 96.9 us -> 87.5 us  [shards(): pl.pallas_call(functools.partial(kernel, n_obs, n_patch, nc, bc), out_sha...]
where the time goes in v2:
time: 89.4 us; the launch traced here: 89.2 us
  Pallas kernels  87.5 us (98%)
  local copies, waits for them, and re-layouts  1.72 us (2%)
    pallas_call x1, Pallas kernels, shards(): pl.pallas_call(functools.partial(kernel, n_obs, n_patch, nc, bc), out_sha...  87.5 us

profile of v2, /device:TPU:0, one launch (start us, length us, event | category | flops | bytes accessed | tf_op | source)
XLA Modules:
  0.0 89.2 jit_solution(758194659658389652)
XLA Ops:
  0.0 87.5 %shard_map.46 = f32[640,128]{1,0:T(8,128)} custom-call(f32[1280,640]{1,0:T(8,128)} %green.1, f32[1280,128]{1,0:T(8,128)} %data.1, s32[3,640]{1,0:T(4,128)} %nb.1, f32[1,128]{1,0:T(1,128)} %bitcast.1), custom_call_target="tpu_custom_call" | custom-call | tf_op jit(solution)/shard_map/pallas_call | solution.py:717
  87.5 1.7 %copy.6 = f32[640,128]{1,0:T(8,128)} copy(f32[640,128]{1,0:T(8,128)} %shard_map.46) | data formatting | bytes 655360

commit v3 on v2

--- a/solution.py
+++ b/solution.py
@@ -13,7 +13,7 @@
 F32 = jnp.float32
 BF16 = jnp.bfloat16
 R = 64
-LAG = 6
+LAG = 8
 
 
 def dot(a, b):
@@ -29,12 +29,12 @@
     return jnp.sum(x, axis=0, keepdims=True)
 
 
-def kernel(n_obs, n_patch, nc, bc, green, data, nb, rw, out,
-           gbuf, gpar, dbuf, ghi, glo, nbp, nbe, lm, lmt,
+def kernel(n_obs, n_patch, nc, bc, green, data, nb_in, rw_in, out,
+           gbuf, gpar, dbuf, ghi, glo, nb, nbp, nbe, rw, lm, lmt,
            cat_d, cat_e, cat_u, lt, lt0,
            d, g, a, wown, wsrc, slip, slp, dp, sq, hsrc, hd, hg, qd, qg,
            s, sr, sl, rl, rr, bb, br, nat, natp, hal, wr, scs, scr, pls, plr, tsrc, tdst,
-           sem_l, sem_r, sem_b, sem_h, sem_w, sem_s, sem_p, sem_n, sem_x, sem_y, sem_g, sem_nb, sem_in):
+           sem_out, sem_l, sem_r, sem_b, sem_h, sem_w, sem_s, sem_p, sem_x, sem_y, sem_g, sem_nb, sem_in):
     rows, cols = gbuf.shape
     E = dbuf.shape[1]
     H = E // 2
@@ -107,15 +107,20 @@
         return (z + i) % nz
 
     def load(i):
-        r0 = pl.multiple_of(i * BAND, BAND)
-        return pltpu.make_async_copy(green.at[pl.ds(r0, BAND)], gbuf.at[pl.ds(r0, BAND)], sem_in.at[i])
-
-    load_data = pltpu.make_async_copy(data, dbuf, sem_in.at[nblk])
+        rs = pl.ds(pl.multiple_of(i * 2 * BAND, 2 * BAND), 2 * BAND)
+        return pltpu.make_async_copy(green.at[rs], gbuf.at[rs], sem_in.at[i])
+
+    load_data = pltpu.make_async_copy(data, dbuf, sem_in.at[RB])
+    load_nb = pltpu.make_async_copy(nb_in, nb, sem_in.at[RB + 1])
+    load_rw = pltpu.make_async_copy(rw_in, rw, sem_in.at[RB + 2])
     load_data.start()
 
-    @pl.loop(0, nblk)
+    @pl.loop(0, RB)
     def _(i):
         load(i).start()
+
+    load_nb.start()
+    load_rw.start()
 
     barrier = pltpu.get_barrier_semaphore()
 
@@ -126,9 +131,6 @@
     @pl.loop(1, n_plane)
     def _(i):
         pl.semaphore_signal(barrier, inc=1, device_id=plane(i), device_id_type=MESH)
-
-    wrow = rw[...]
-    weight = jnp.where(mine(1), wrow, roll(wrow))
 
     load_data.wait()
 
@@ -146,19 +148,25 @@
             ghi[pl.ds(r0, BAND), pl.ds(c0, BAND)] = hi[:, j * BAND:(j + 1) * BAND]
             glo[pl.ds(r0, BAND), pl.ds(c0, BAND)] = lo[:, j * BAND:(j + 1) * BAND]
 
-    @pl.loop(0, nblk)
+    @pl.loop(0, RB)
     def _(i):
         load(i).wait()
-        put_green(gbuf, i, c)
+        put_green(gbuf, 2 * i, c)
+        put_green(gbuf, 2 * i + 1, c)
+
+    load_nb.wait()
+    load_rw.wait()
+    wrow = rw[...]
+    weight = jnp.where(mine(1), wrow, roll(wrow))
 
     pl.semaphore_wait(barrier, nz - 1 + n_plane - 1)
 
-    ncopy = rcopy(nb, nbp, pair(sem_nb), at(obs, partner))
+    ncopy = rcopy(nb, nbp, (sem_nb.at[0], sem_nb.at[1]), at(obs, partner))
     ncopy.start()
 
     def gcopy(i):
-        r0 = pl.multiple_of(i * BAND, BAND)
-        return rcopy(gbuf.at[pl.ds(r0, BAND)], gpar.at[pl.ds(r0, BAND)], pair(sem_g, i), at(obs, partner))
+        rs = pl.ds(i * (rows // 2), rows // 2)
+        return rcopy(gbuf.at[rs], gpar.at[rs], (sem_out.at[3], sem_g.at[i]), at(obs, partner))
 
     def build_laplace():
         ncopy.wait_recv()
@@ -219,7 +227,7 @@
         return at(obs + bit * (1 - 2 * ((obs // bit) % 2)), pat)
 
     def bcopy(b, p, j):
-        return rcopy(bb.at[b, p, j], br.at[b, p, j], pair(sem_b, b, p, j), bit_partner(p, j))
+        return rcopy(bb.at[b, p, j], br.at[b, p, j], (sem_out.at[2], sem_b.at[b % 2, p, j]), bit_partner(p, j))
 
     def product(b, m):
         if b == 0:
@@ -254,22 +262,19 @@
             finish(j, bb[b, nbit - 1, j] + br[b, nbit - 1, j])
 
     def backward_sent(b):
-        for p in range(nbit):
-            @pl.loop(0, bc)
-            def _(j):
-                bcopy(b, p, j).wait_send()
+        rcopy(bb.at[b], br.at[b], (sem_out.at[2], sem_b.at[0, 0, 0]), at(obs, partner)).wait_send()
 
     def rcopy_up(it, src, k):
-        return rcopy(src.at[k], rl.at[it, k], pair(sem_l, it, k), at(obs, pat + 2))
+        return rcopy(src.at[k], rl.at[it, k], (sem_out.at[0], sem_l.at[it % 2, k]), at(obs, pat + 2))
 
     def rcopy_down(it, src, k):
-        return rcopy(src.at[k], rr.at[it, k], pair(sem_r, it, k), at(obs, pat - 2))
+        return rcopy(src.at[k], rr.at[it, k], (sem_out.at[1], sem_r.at[it % 2, k]), at(obs, pat - 2))
 
     def hcopy_r(it):
-        return rcopy(hsrc.at[it, 0], hal.at[it, 0], pair(sem_h, it, 0), at(obs, pat + 2))
+        return rcopy(hsrc.at[it, 0], hal.at[it, 0], (sem_out.at[4], sem_h.at[it % 2, 0]), at(obs, pat + 2))
 
     def hcopy_l(it):
-        return rcopy(hsrc.at[it, 1], hal.at[it, 1], pair(sem_h, it, 1), at(obs, pat - 2))
+        return rcopy(hsrc.at[it, 1], hal.at[it, 1], (sem_out.at[5], sem_h.at[it % 2, 1]), at(obs, pat - 2))
 
     def put_lt(m):
         x = qd[pl.ds(m * per, per)].reshape(BAND, E)
@@ -384,15 +389,13 @@
                 reg_sums()
 
     def forward_sent(it):
-        @pl.loop(0, nc)
-        def _(k):
-            @pl.when(up)
-            def _():
-                rcopy_up(it, sr, k).wait_send()
-
-            @pl.when(down)
-            def _():
-                rcopy_down(it, sl, k).wait_send()
+        @pl.when(up)
+        def _():
+            rcopy(sr, rl.at[it], (sem_out.at[0], sem_l.at[0, 0]), at(obs, partner)).wait_send()
+
+        @pl.when(down)
+        def _():
+            rcopy(sl, rr.at[it], (sem_out.at[1], sem_r.at[0, 0]), at(obs, partner)).wait_send()
 
         @pl.when(up)
         def _():
@@ -433,10 +436,10 @@
         return weight * jnp.where(low(BAND), banded(lm, cat_e, i), banded(lm, cat_e, CB + i))
 
     def wcopy_l(it):
-        return rcopy(wsrc.at[it, 0], wr.at[it, 1], pair(sem_w, it, 1), at(obs, pat - 2))
+        return rcopy(wsrc.at[it, 0], wr.at[it, 1], (sem_out.at[7], sem_w.at[it, 1]), at(obs, pat - 2))
 
     def wcopy_r(it):
-        return rcopy(wsrc.at[it, 1], wr.at[it, 0], pair(sem_w, it, 0), at(obs, pat + 2))
+        return rcopy(wsrc.at[it, 1], wr.at[it, 0], (sem_out.at[6], sem_w.at[it, 0]), at(obs, pat + 2))
 
     def reg_work(it):
         laplace()
@@ -481,6 +484,7 @@
 
         wown[0:BAND, :] += jnp.where(low(BAND), widen(wr[it, 0]), 0.0)
         wown[cols - BAND:cols, :] += jnp.where(low(BAND), 0.0, widen(wr[it, 1]))
+        reg_sent(it)
 
     def reg_sent(it):
         @pl.when(has_l)
@@ -491,31 +495,28 @@
         def _():
             wcopy_r(it).wait_send()
 
-    def scopy(it, slot, q):
-        return rcopy(scs.at[it], scr.at[it, slot], (sem_s.at[0, it, q], sem_s.at[1, it, slot]), at(obs, q * 2 + c))
+    def scopy(it, q):
+        return rcopy(scs.at[it], scr.at[it, z], (sem_out.at[8], sem_s.at[it]), at(obs, q * 2 + c))
+
+    def sums_all(it):
+        part = scr.at[it, pl.ds(0, nz - 1)]
+        return rcopy(part, part, (sem_out.at[8], sem_s.at[it]), at(obs, partner))
 
     def sums_start(it):
         scr[it, z] = scs[it]
 
         @pl.loop(1, nz)
         def _(i):
-            scopy(it, z, zpeer(i)).start()
+            scopy(it, zpeer(i)).start()
 
     def sums_end(it):
-        @pl.loop(1, nz)
-        def _(i):
-            scopy(it, zpeer(i), zpeer(i)).wait_recv()
-
+        sums_all(it).wait_recv()
+        sums_all(it).wait_send()
         return fold(jnp.sum(scr[it], axis=0))
 
-    def sums_sent(it):
-        @pl.loop(1, nz)
-        def _(i):
-            scopy(it, z, zpeer(i)).wait_send()
-
-    def pcopy(o, q, i):
+    def pcopy(i):
         po, pp = plane(i)
-        return rcopy(pls, plr.at[o, q], (sem_p.at[i], sem_n.at[o, q]), (po, pp))
+        return rcopy(pls, plr.at[obs * 2 + c], (sem_p.at[0], sem_p.at[1]), (po, pp))
 
     norms = []
 
@@ -561,20 +562,20 @@
         return step, ratio
 
     def xcopy(j):
-        return rcopy(nat.at[j], natp.at[j], pair(sem_x, j), at(obs, partner))
+        return rcopy(nat.at[j], natp.at[j], (sem_out.at[9], sem_x.at[j]), at(obs, partner))
 
     def first_hook():
-        @pl.loop(0, nblk)
-        def _(i):
-            gcopy(i).start()
-
+        gcopy(0).start()
+        gcopy(1).start()
         clear()
 
     def first_late():
-        @pl.loop(0, nblk)
-        def _(i):
-            gcopy(i).wait_recv()
-            put_green(gpar, i, other)
+        for h in range(2):
+            gcopy(h).wait_recv()
+
+            @pl.loop(h * nblk // 2, (h + 1) * nblk // 2)
+            def _(i):
+                put_green(gpar, i, other)
 
     def first_finish(j, x):
         nat[j] = x
@@ -624,35 +625,20 @@
     last = ITERS - 1
     norm = norms[-1]
     pls[...] = sq[...]
-    plr[obs, c] = sq[...]
+    plr[obs * 2 + c] = sq[...]
 
     @pl.loop(1, n_plane)
     def _(i):
-        pcopy(obs, c, i).start()
-
-    @pl.loop(1, nz)
-    def _(i):
-        scopy(last, zpeer(i), zpeer(i)).wait_recv()
+        pcopy(i).start()
 
     tsrc[0:1, :] = norm
-    tsrc[1:2, :] = fold(rowsum(jnp.sum(scr[last], axis=0)))
+    tsrc[1:2, :] = rowsum(sums_end(last))
     tcopy.start()
 
     forward_sent(last)
-    for it in range(ITERS):
-        sums_sent(it)
-    for it in range(ITERS - 1):
-        reg_sent(it)
     ncopy.wait_send()
-
-    @pl.loop(0, nblk)
-    def _(i):
-        gcopy(i).wait_send()
-
-    @pl.loop(0, bc)
-    def _(j):
-        xcopy(j).wait_send()
-
+    rcopy(gbuf, gpar, (sem_out.at[3], sem_g.at[0]), at(obs, partner)).wait_send()
+    rcopy(nat, natp, (sem_out.at[9], sem_x.at[0]), at(obs, partner)).wait_send()
     ycopy(0).wait_recv()
     ycopy(1).wait_recv()
     ycopy(0).wait_send()
@@ -665,21 +651,17 @@
     tcopy.wait_recv()
     tcopy.wait_send()
 
-    @pl.loop(1, n_plane)
-    def _(i):
-        q = (obs * 2 + c + i) % n_plane
-        pcopy(q // 2, q % 2, i).wait_recv()
+    part = plr.at[pl.ds(0, n_plane - 1)]
+    rcopy(part, part, (sem_p.at[0], sem_p.at[1]), at(obs, partner)).wait_recv()
 
     def step_of(t, q):
-        return t[0:1, :] / (fold(rowsum(jnp.sum(plr[:, q], axis=0))) + t[1:2, :])
+        return t[0:1, :] / (fold(sum(rowsum(plr[2 * o + q]) for o in range(n_obs))) + t[1:2, :])
 
     step = jnp.where(mine(1), step_of(tsrc, c), step_of(tdst, other))
 
     out[...] = slip[...] + step * d[...]
 
-    @pl.loop(1, n_plane)
-    def _(i):
-        pcopy(obs, c, i).wait_send()
+    rcopy(part, part, (sem_p.at[0], sem_p.at[1]), at(obs, partner)).wait_send()
 
 
 def shards(green, data, neighbours, reg_weight):
@@ -696,7 +678,7 @@
     scratch = [
         V((rows, cols), F32), V((rows, cols), F32), V((rows, E), F32),
         V((rows, 2 * cols), BF16), V((rows, 2 * cols), BF16),
-        V(neighbours.shape, jnp.int32), V((8, (NB + 4) * BAND), jnp.int32),
+        V(neighbours.shape, jnp.int32), V(neighbours.shape, jnp.int32), V((8, (NB + 4) * BAND), jnp.int32), V((1, E), F32),
         V((NB * BAND, 3 * BAND), BF16), V(((NB + 2) * BAND, 3 * BAND), BF16),
         V((2 * cols, 3 * E), BF16), V(((NB + 2) * BAND, 2 * E), BF16), V(((NB + 4) * BAND, 2 * E), BF16),
         V((E, rows), BF16), V((2 * E, rows), BF16),
@@ -709,15 +691,14 @@
         V((bc, R, E), F32), V((bc, R, E), F32),
         V((ITERS, 2, R, E), F32), V((ITERS - 1, 2, R, E), F32),
         V((ITERS, 8, E), F32), V((ITERS, nz, 8, E), F32),
-        V((8, E), F32), V((n_obs, 2, 8, E), F32), V((8, E), F32), V((8, E), F32),
-        D((2, ITERS, nc)), D((2, ITERS, nc)), D((2, ITERS, nbit, bc)), D((2, ITERS, 2)), D((2, ITERS - 1, 2)),
-        D((2, ITERS, nz)), D((2 * n_obs,)), D((n_obs, 2)), D((2, bc)), D((2, 3)), D((2, nblk)), D((2,)),
-        D((nblk + 1,)),
+        V((8, E), F32), V((2 * n_obs, 8, E), F32), V((8, E), F32), V((8, E), F32),
+        D((10,)), D((2, nc)), D((2, nc)), D((2, nbit, bc)), D((2, 2)), D((ITERS - 1, 2)),
+        D((ITERS,)), D((2,)), D((bc,)), D((2, 3)), D((2,)), D((2,)), D((rows // (2 * BAND) + 3,)),
     ]
     return pl.pallas_call(
         functools.partial(kernel, n_obs, n_patch, nc, bc),
         out_shape=jax.ShapeDtypeStruct((cols, E), F32),
-        in_specs=[pl.BlockSpec(memory_space=pl.ANY)] * 2 + [pl.BlockSpec(memory_space=pltpu.VMEM)] * 2,
+        in_specs=[pl.BlockSpec(memory_space=pl.ANY)] * 4,
         out_specs=pl.BlockSpec(memory_space=pltpu.VMEM),
         scratch_shapes=scratch,
         compiler_params=pltpu.CompilerParams(

time: 89.4 us -> 84.4 us (0.944)
  Pallas kernels: 87.5 us -> 82.5 us
    pallas_call x1, Pallas kernels: 87.5 us -> 82.5 us  [shards(): pl.pallas_call(functools.partial(kernel, n_obs, n_patch, nc, bc), out_sha...]
where the time goes in v3:
time: 84.4 us; the launch traced here: 84.3 us
  Pallas kernels  82.5 us (98%)
  local copies, waits for them, and re-layouts  1.72 us (2%)
    pallas_call x1, Pallas kernels, shards(): pl.pallas_call(functools.partial(kernel, n_obs, n_patch, nc, bc), out_sha...  82.5 us
    unnamed x1, local copies, waits for them, and re-layouts  1.72 us

profile of v3, /device:TPU:0, one launch (start us, length us, event | category | flops | bytes accessed | tf_op | source)
XLA Modules:
  0.0 84.3 jit_solution(7594366542261724973)
XLA Ops:
  0.0 82.5 %shard_map.46 = f32[640,128]{1,0:T(8,128)} custom-call(f32[1280,640]{1,0:T(8,128)} %green.1, f32[1280,128]{1,0:T(8,128)} %data.1, s32[3,640]{1,0:T(4,128)} %nb_in.1, f32[1,128]{1,0:T(1,128)} %bitcast.1), custom_call_target="tpu_custom_call" | custom-call | tf_op jit(solution)/shard_map/pallas_call | solution.py:698
  82.6 1.7 %copy.6 = f32[640,128]{1,0:T(8,128)} copy(f32[640,128]{1,0:T(8,128)} %shard_map.46) | data formatting | bytes 655360

commit v4 on v3

--- a/solution.py
+++ b/solution.py
@@ -13,6 +13,7 @@
 F32 = jnp.float32
 BF16 = jnp.bfloat16
 R = 64
+HB = BAND // 2
 LAG = 8
 
 
@@ -33,8 +34,8 @@
            gbuf, gpar, dbuf, ghi, glo, nb, nbp, nbe, rw, lm, lmt,
            cat_d, cat_e, cat_u, lt, lt0,
            d, g, a, wown, wsrc, slip, slp, dp, sq, hsrc, hd, hg, qd, qg,
-           s, sr, sl, rl, rr, bb, br, nat, natp, hal, wr, scs, scr, pls, plr, tsrc, tdst,
-           sem_out, sem_l, sem_r, sem_b, sem_h, sem_w, sem_s, sem_p, sem_x, sem_y, sem_g, sem_nb, sem_in):
+           s, sr, sl, rl, rr, bb, br, nat, natp, hal, wr, scs, scr, zsq, pls, plr, tsrc, tdst,
+           sem_out, sem_l, sem_r, sem_b, sem_h, sem_w, sem_s, sem_p, sem_x, sem_y, sem_g, sem_nb, sem_in, sem_zs):
     rows, cols = gbuf.shape
     E = dbuf.shape[1]
     H = E // 2
@@ -55,6 +56,7 @@
     up, down = has_r, has_l
     inner = up & down
     n_plane = 2 * n_obs
+    za, zb = nz // 2 - 1, nz // 2
 
     def lanes(n):
         return lax.broadcasted_iota(jnp.int32, (n, E), 1)
@@ -165,8 +167,8 @@
     ncopy.start()
 
     def gcopy(i):
-        rs = pl.ds(i * (rows // 2), rows // 2)
-        return rcopy(gbuf.at[rs], gpar.at[rs], (sem_out.at[3], sem_g.at[i]), at(obs, partner))
+        rs = pl.ds(i * BAND, BAND)
+        return rcopy(gbuf.at[rs], gpar.at[rs], (sem_out.at[3], sem_g.at[i // (nblk // 2)]), at(obs, partner))
 
     def build_laplace():
         ncopy.wait_recv()
@@ -203,7 +205,7 @@
     def clear():
         scs[...] = jnp.zeros((ITERS, 8, E), F32)
         zero_c = jnp.zeros((nc, R, E), F32)
-        zero_h = jnp.zeros((R, E), F32)
+        zero_h = jnp.zeros((HB, E), F32)
 
         @pl.when(z == 0)
         def _():
@@ -240,11 +242,33 @@
         y = y[:H] + y[H:] + dot(lt[0:H, :], glo[:, pl.ds(c0, 2 * BAND)])
         return jnp.concatenate([y[:, :BAND], y[:, BAND:]], axis=0).T
 
+    def xcopy(m):
+        return rcopy(nat.at[m], natp.at[m], (sem_out.at[9], sem_x.at[m]), at(obs, partner))
+
+    gcopy(0).start()
+
     def backward(b, hook, late, finish):
         for m in range(CB):
-            bb[b, 0, m * per:(m + 1) * per] = product(b, m).reshape(per, R, E)
+            y = product(b, m)
+            if b == 0:
+                nat[m] = y
+                xcopy(m).start()
+                gcopy(m + 1).start()
+                continue
+            bb[b, 0, m * per:(m + 1) * per] = y.reshape(per, R, E)
             for k in range(per):
                 bcopy(b, 0, m * per + k).start()
+
+        if b == 0:
+            for i in range(CB + 1, nblk):
+                gcopy(i).start()
+            pl.when(c == 0)(build_laplace)
+            for m in range(CB):
+                xcopy(m).wait_recv()
+                y = jnp.where(mine(BAND), nat[m], roll(natp[m]))
+                bb[b, 0, m * per:(m + 1) * per] = y.reshape(per, R, E)
+                for k in range(per):
+                    bcopy(b, 0, m * per + k).start()
 
         hook()
         for p in range(1, nbit):
@@ -290,14 +314,18 @@
         last = it == ITERS - 1
         v = a if it else g
         x = v[cols - BAND:cols, :]
-        hsrc[it, 0] = jnp.where(low(R), roll(x[:R]), x[R:])
+        hsrc[it, 0] = jnp.where(low(HB), roll(x[:HB]), x[HB:])
         x = v[0:BAND, :]
-        hsrc[it, 1] = jnp.where(low(R), x[:R], roll(x[R:]))
+        hsrc[it, 1] = jnp.where(low(HB), x[:HB], roll(x[HB:]))
 
         @pl.when(up & down)
         def _():
             hcopy_r(it).start()
             hcopy_l(it).start()
+
+        if last:
+            forward_last(sums, hook)
+            return
 
         def group(m):
             r0 = m * 2 * BAND
@@ -363,30 +391,140 @@
                     step, ratio = scalars
                     rest = qg[kt] - step * total
                     total = rest + ratio * qd[kt]
-                if last:
-                    sq[...] += jnp.sum((total * total).reshape(R // 8, 8, E), axis=0)
-                else:
-                    qg[kt] = rest if it else total
-                    qd[kt] = total
-
-                    @pl.when(kt % per == per - 1)
-                    def _():
-                        put_lt(kt // per)
-
-        if last:
-            sq[...] = jnp.zeros((8, E), F32)
+                qg[kt] = rest if it else total
+                qd[kt] = total
+
+                @pl.when(kt % per == per - 1)
+                def _():
+                    put_lt(kt // per)
+
         pl.loop(LAG, LAG * (nz // 2))(functools.partial(chain, ends=False))
         scalars = hook()
 
         @pl.when(jnp.logical_not(inner))
         def _():
-            reg_sums() if last else reg_work(it)
+            reg_work(it)
 
         pl.loop(LAG * (nz // 2), nc + LAG * (nz - 1))(chain)
-        if last:
-            @pl.when(inner)
-            def _():
-                reg_sums()
+
+    def forward_last(sums, hook):
+        it = ITERS - 1
+        low_side = z <= za
+
+        def order(i, n):
+            return jnp.where(low_side, n - 1 - i, i)
+
+        def group(i):
+            m = order(i, RB)
+            rs = pl.ds(pl.multiple_of(m * 2 * BAND, 2 * BAND), 2 * BAND)
+            y = dot(ghi[rs, :], cat_d[:, 0:2 * E])
+            y = y[:, :E] + y[:, E:] + dot(glo[rs, :], cat_d[:, 2 * E:3 * E])
+            y = jnp.where(low(BAND), y[:BAND], y[BAND:])
+            s[pl.ds(m * per, per)] = y.reshape(per, R, E)
+            for j in range(per):
+                k = m * per + order(j, per)
+
+                @pl.when((z == 0) & ((z < za) | (k >= nc // 2)))
+                def _():
+                    rcopy_up(it, s, k).start()
+
+                @pl.when((z == nz - 1) & ((z > zb) | (k < nc // 2)))
+                def _():
+                    rcopy_down(it, s, k).start()
+
+        group(0)
+        sums()
+
+        @pl.when(up & (z == 0))
+        def _():
+            hcopy_r(it).start()
+
+        @pl.when(down & (z == nz - 1))
+        def _():
+            hcopy_l(it).start()
+
+        for i in range(1, RB):
+            group(i)
+        backward_sent(it)
+        sq[...] = jnp.zeros((8, E), F32)
+
+        def move(n0, n1):
+            @pl.loop(n0, n1)
+            def _(i):
+                k = order(i, nc)
+
+                @pl.when(low_side & down)
+                def _():
+                    rcopy_up(it, sr, k).wait_recv()
+
+                    @pl.when((z < za) | (k >= nc // 2))
+                    def _():
+                        sr[k] = rl[it, k] + s[k]
+                        rcopy_up(it, sr, k).start()
+
+                @pl.when(jnp.logical_not(low_side) & up)
+                def _():
+                    rcopy_down(it, sl, k).wait_recv()
+
+                    @pl.when((z > zb) | (k < nc // 2))
+                    def _():
+                        sl[k] = rr[it, k] + s[k]
+                        rcopy_down(it, sl, k).start()
+
+        half = nc - nc // 2
+        move(0, half)
+        step, ratio = hook()
+        move(half, nc)
+
+        def ends(k):
+            total = rl[it, k] + s[k] + rr[it, k]
+            total = qg[k] - step * total + ratio * qd[k]
+            sq[...] += jnp.sum((total * total).reshape(R // 8, 8, E), axis=0)
+
+        @pl.when(z == za)
+        def _():
+            @pl.loop(0, nc // 2)
+            def _(k):
+                rcopy_down(it, sl, k).wait_recv()
+                ends(k)
+
+        @pl.when(z == zb)
+        def _():
+            @pl.loop(nc // 2, nc)
+            def _(k):
+                rcopy_up(it, sr, k).wait_recv()
+                ends(k)
+
+    def last_sent():
+        it = ITERS - 1
+
+        def wait(buf, sem, n):
+            part = buf.at[pl.ds(0, n)]
+            rcopy(part, part, (sem, sem_p.at[2]), at(obs, partner)).wait_send()
+
+        @pl.when(z < za)
+        def _():
+            wait(sr, sem_out.at[0], nc)
+
+        @pl.when(z == za)
+        def _():
+            wait(sr, sem_out.at[0], nc - nc // 2)
+
+        @pl.when(z == zb)
+        def _():
+            wait(sl, sem_out.at[1], nc // 2)
+
+        @pl.when(z > zb)
+        def _():
+            wait(sl, sem_out.at[1], nc)
+
+        @pl.when(up)
+        def _():
+            hcopy_r(it).wait_send()
+
+        @pl.when(down)
+        def _():
+            hcopy_l(it).wait_send()
 
     def forward_sent(it):
         @pl.when(up)
@@ -451,7 +589,7 @@
 
         for side, j in ((0, 0), (1, NB + 1)):
             y = banded(lmt, cat_u, j)
-            wsrc[it, side] = weight * jnp.where(low(R), y[:R], y[R:])
+            wsrc[it, side] = weight * jnp.where(low(HB), y[:HB], y[HB:])
 
         @pl.when(has_l)
         def _():
@@ -561,25 +699,17 @@
             ycopy(1).start()
         return step, ratio
 
-    def xcopy(j):
-        return rcopy(nat.at[j], natp.at[j], (sem_out.at[9], sem_x.at[j]), at(obs, partner))
-
     def first_hook():
-        gcopy(0).start()
-        gcopy(1).start()
         clear()
 
     def first_late():
         for h in range(2):
-            gcopy(h).wait_recv()
+            rs = pl.ds(h * (rows // 2), rows // 2)
+            rcopy(gbuf.at[rs], gpar.at[rs], (sem_out.at[3], sem_g.at[h]), at(obs, partner)).wait_recv()
 
             @pl.loop(h * nblk // 2, (h + 1) * nblk // 2)
             def _(i):
                 put_green(gpar, i, other)
-
-    def first_finish(j, x):
-        nat[j] = x
-        xcopy(j).start()
 
     def put_operand(ref, i):
         top, bot = both(ref[pl.ds(pl.multiple_of(i * BAND, BAND), BAND), :])
@@ -587,13 +717,8 @@
         put_cat(cat_d, r0, top, True)
         put_cat(cat_d, pl.multiple_of(r0 + BAND, BAND), bot, True)
 
-    backward(0, first_hook, first_late, first_finish)
-
-    @pl.loop(0, bc)
-    def _(j):
-        xcopy(j).wait_recv()
+    def first_finish(j, x):
         r0 = pl.multiple_of(j * R, R)
-        x = jnp.where(mine(R), nat[j], roll(natp[j]))
         g[pl.ds(r0, R), :] = x
         d[pl.ds(r0, R), :] = x
 
@@ -601,7 +726,7 @@
         def _():
             put_operand(g, j // per)
 
-    pl.when(c == 0)(build_laplace)
+    backward(0, first_hook, first_late, first_finish)
     forward(0, lambda: None, lambda: pl.when(c == 1)(build_laplace), first)
     for it in range(1, ITERS):
         def hook(it=it):
@@ -624,8 +749,35 @@
 
     last = ITERS - 1
     norm = norms[-1]
-    pls[...] = sq[...]
-    plr[obs * 2 + c] = sq[...]
+    mid = (z == za) | (z == zb)
+
+    def zcopy(i):
+        q = zpeer(i)
+        return rcopy(sq, zsq.at[z - za], (sem_zs.at[0], sem_p.at[2 + z - za]), at(obs, q * 2 + c))
+
+    def zwait(slot):
+        rcopy(sq, zsq.at[slot], (sem_zs.at[0], sem_p.at[2 + slot]), at(obs, partner)).wait_recv()
+
+    @pl.when(mid)
+    def _():
+        zsq[z - za] = sq[...]
+
+        @pl.loop(1, nz)
+        def _(i):
+            zcopy(i).start()
+
+    reg_sums()
+
+    @pl.when(z != za)
+    def _():
+        zwait(0)
+
+    @pl.when(z != zb)
+    def _():
+        zwait(1)
+
+    pls[...] = zsq[0] + zsq[1]
+    plr[obs * 2 + c] = pls[...]
 
     @pl.loop(1, n_plane)
     def _(i):
@@ -635,7 +787,13 @@
     tsrc[1:2, :] = rowsum(sums_end(last))
     tcopy.start()
 
-    forward_sent(last)
+    last_sent()
+
+    @pl.when(mid)
+    def _():
+        part = scr.at[last, pl.ds(0, nz - 1)]
+        rcopy(part, part, (sem_zs.at[0], sem_p.at[2]), at(obs, partner)).wait_send()
+
     ncopy.wait_send()
     rcopy(gbuf, gpar, (sem_out.at[3], sem_g.at[0]), at(obs, partner)).wait_send()
     rcopy(nat, natp, (sem_out.at[9], sem_x.at[0]), at(obs, partner)).wait_send()
@@ -682,22 +840,22 @@
         V((NB * BAND, 3 * BAND), BF16), V(((NB + 2) * BAND, 3 * BAND), BF16),
         V((2 * cols, 3 * E), BF16), V(((NB + 2) * BAND, 2 * E), BF16), V(((NB + 4) * BAND, 2 * E), BF16),
         V((E, rows), BF16), V((2 * E, rows), BF16),
-        V((cols, E), F32), V((cols, E), F32), V((cols, E), F32), V((cols, E), F32), V((ITERS - 1, 2, R, E), F32),
+        V((cols, E), F32), V((cols, E), F32), V((cols, E), F32), V((cols, E), F32), V((ITERS - 1, 2, HB, E), F32),
         V((cols, E), F32), V((cols, E), F32), V((cols, E), F32), V((8, E), F32),
-        V((ITERS, 2, R, E), F32), V((2, R, E), F32), V((2, R, E), F32), V((nc, R, E), F32), V((nc, R, E), F32),
+        V((ITERS, 2, HB, E), F32), V((2, HB, E), F32), V((2, HB, E), F32), V((nc, R, E), F32), V((nc, R, E), F32),
         V((nc, R, E), F32), V((nc, R, E), F32), V((nc, R, E), F32),
         V((ITERS, nc, R, E), F32), V((ITERS, nc, R, E), F32),
         V((ITERS, nbit, bc, R, E), F32), V((ITERS, nbit, bc, R, E), F32),
-        V((bc, R, E), F32), V((bc, R, E), F32),
-        V((ITERS, 2, R, E), F32), V((ITERS - 1, 2, R, E), F32),
+        V((cols // BAND, BAND, E), F32), V((cols // BAND, BAND, E), F32),
+        V((ITERS, 2, HB, E), F32), V((ITERS - 1, 2, HB, E), F32),
         V((ITERS, 8, E), F32), V((ITERS, nz, 8, E), F32),
-        V((8, E), F32), V((2 * n_obs, 8, E), F32), V((8, E), F32), V((8, E), F32),
+        V((2, 8, E), F32), V((8, E), F32), V((2 * n_obs, 8, E), F32), V((8, E), F32), V((8, E), F32),
         D((10,)), D((2, nc)), D((2, nc)), D((2, nbit, bc)), D((2, 2)), D((ITERS - 1, 2)),
-        D((ITERS,)), D((2,)), D((bc,)), D((2, 3)), D((2,)), D((2,)), D((rows // (2 * BAND) + 3,)),
+        D((ITERS,)), D((4,)), D((cols // BAND,)), D((2, 3)), D((2,)), D((2,)), D((rows // (2 * BAND) + 3,)), D((1,)),
     ]
     return pl.pallas_call(
         functools.partial(kernel, n_obs, n_patch, nc, bc),
-        out_shape=jax.ShapeDtypeStruct((cols, E), F32),
+        out_shape=pltpu.VMEM((cols, E), F32),
         in_specs=[pl.BlockSpec(memory_space=pl.ANY)] * 4,
         out_specs=pl.BlockSpec(memory_space=pltpu.VMEM),
         scratch_shapes=scratch,

time: 84.4 us -> 80.6 us (0.955)
  Pallas kernels: 82.5 us -> 79.7 us
  local copies, waits for them, and re-layouts: 1.72 us -> 0.73 us
    pallas_call x1, Pallas kernels: 82.5 us -> 79.7 us  [shards(): pl.pallas_call(functools.partial(kernel, n_obs, n_patch, nc, bc), out_sha...]
    unnamed x1, local copies, waits for them, and re-layouts: 1.72 us -> 0.73 us
where the time goes in v4:
time: 80.6 us; the launch traced here: 80.4 us
  Pallas kernels  79.7 us (99%)
    pallas_call x1, Pallas kernels, shards(): pl.pallas_call(functools.partial(kernel, n_obs, n_patch, nc, bc), out_sha...  79.7 us

profile of v4, /device:TPU:0, one launch (start us, length us, event | category | flops | bytes accessed | tf_op | source)
XLA Modules:
  0.0 80.4 jit_solution(14760038369793076165)
XLA Ops:
  0.0 79.7 %shard_map.46 = f32[640,128]{1,0:T(8,128)S(1)} custom-call(f32[1280,640]{1,0:T(8,128)} %green.1, f32[1280,128]{1,0:T(8,128)} %data.1, s32[3,640]{1,0:T(4,128)} %nb_in.1, f32[1,128]{1,0:T(1,128)} %bitcast.1), custom_call_target="tpu_custom_call" | custom-call | tf_op jit(solution)/shard_map/pallas_call | solution.py:856
  79.7 0.7 copy.6

commit v5 on v4

--- a/solution.py
+++ b/solution.py
@@ -24,6 +24,10 @@
 def split(x):
     hi = x.astype(BF16)
     return hi, (x - hi.astype(F32)).astype(BF16)
+
+
+def batches(n):
+    return [[0]] + [list(range(i, min(i + 2, n))) for i in range(1, n, 2)]
 
 
 def rowsum(x):
@@ -161,11 +165,7 @@
     wrow = rw[...]
     weight = jnp.where(mine(1), wrow, roll(wrow))
 
-    pl.semaphore_wait(barrier, nz - 1 + n_plane - 1)
-
     ncopy = rcopy(nb, nbp, (sem_nb.at[0], sem_nb.at[1]), at(obs, partner))
-    ncopy.start()
-
     def gcopy(i):
         rs = pl.ds(i * BAND, BAND)
         return rcopy(gbuf.at[rs], gpar.at[rs], (sem_out.at[3], sem_g.at[i // (nblk // 2)]), at(obs, partner))
@@ -245,22 +245,30 @@
     def xcopy(m):
         return rcopy(nat.at[m], natp.at[m], (sem_out.at[9], sem_x.at[m]), at(obs, partner))
 
-    gcopy(0).start()
+    def enter():
+        pl.semaphore_wait(barrier, nz - 1 + n_plane - 1)
+        ncopy.start()
+        gcopy(0).start()
 
     def backward(b, hook, late, finish):
-        for m in range(CB):
-            y = product(b, m)
-            if b == 0:
-                nat[m] = y
-                xcopy(m).start()
-                gcopy(m + 1).start()
-                continue
-            bb[b, 0, m * per:(m + 1) * per] = y.reshape(per, R, E)
-            for k in range(per):
-                bcopy(b, 0, m * per + k).start()
+        for ms in batches(CB) if b else ([0, 1], range(2, CB)):
+            for m in ms:
+                y = product(b, m)
+                if b == 0:
+                    nat[m] = y
+                else:
+                    bb[b, 0, m * per:(m + 1) * per] = y.reshape(per, R, E)
+            if b == 0 and ms[0] == 0:
+                enter()
+            for m in ms:
+                if b == 0:
+                    xcopy(m).start()
+                else:
+                    for k in range(per):
+                        bcopy(b, 0, m * per + k).start()
 
         if b == 0:
-            for i in range(CB + 1, nblk):
+            for i in range(1, nblk):
                 gcopy(i).start()
             pl.when(c == 0)(build_laplace)
             for m in range(CB):
@@ -333,16 +341,20 @@
             y = y[:, :E] + y[:, E:] + dot(glo[r0:r0 + 2 * BAND, :], cat_d[:, 2 * E:3 * E])
             y = jnp.where(low(BAND), y[:BAND], y[BAND:])
             s[m * per:(m + 1) * per] = y.reshape(per, R, E)
-            for k in range(per):
-                @pl.when(z == 0)
-                def _():
-                    rcopy_up(it, s, m * per + k).start()
-
-                @pl.when(z == nz - 1)
-                def _():
-                    rcopy_down(it, s, m * per + k).start()
+
+        def send(ms):
+            @pl.when(z == 0)
+            def _():
+                for k in range(ms[0] * per, (ms[-1] + 1) * per):
+                    rcopy_up(it, s, k).start()
+
+            @pl.when(z == nz - 1)
+            def _():
+                for k in range(ms[0] * per, (ms[-1] + 1) * per):
+                    rcopy_down(it, s, k).start()
 
         group(0)
+        send([0])
         sums()
 
         @pl.when(up & (z == 0))
@@ -353,8 +365,10 @@
         def _():
             hcopy_l(it).start()
 
-        for m in range(1, RB):
-            group(m)
+        for ms in batches(RB)[1:]:
+            for m in ms:
+                group(m)
+            send(ms)
         after()
         backward_sent(it)
 
@@ -421,8 +435,10 @@
             y = y[:, :E] + y[:, E:] + dot(glo[rs, :], cat_d[:, 2 * E:3 * E])
             y = jnp.where(low(BAND), y[:BAND], y[BAND:])
             s[pl.ds(m * per, per)] = y.reshape(per, R, E)
-            for j in range(per):
-                k = m * per + order(j, per)
+
+        def send(ms):
+            for i in range(ms[0] * per, (ms[-1] + 1) * per):
+                k = order(i, nc)
 
                 @pl.when((z == 0) & ((z < za) | (k >= nc // 2)))
                 def _():
@@ -433,6 +449,7 @@
                     rcopy_down(it, s, k).start()
 
         group(0)
+        send([0])
         sums()
 
         @pl.when(up & (z == 0))
@@ -443,8 +460,10 @@
         def _():
             hcopy_l(it).start()
 
-        for i in range(1, RB):
-            group(i)
+        for ms in batches(RB)[1:]:
+            for i in ms:
+                group(i)
+            send(ms)
         backward_sent(it)
         sq[...] = jnp.zeros((8, E), F32)
 

time: 80.6 us -> 79.1 us (0.981)
  Pallas kernels: 79.7 us -> 78.2 us
    pallas_call x1, Pallas kernels: 79.7 us -> 78.2 us  [shards(): pl.pallas_call(functools.partial(kernel, n_obs, n_patch, nc, bc), out_sha...]
where the time goes in v5:
time: 79.1 us; the launch traced here: 79 us
  Pallas kernels  78.2 us (99%)
    pallas_call x1, Pallas kernels, shards(): pl.pallas_call(functools.partial(kernel, n_obs, n_patch, nc, bc), out_sha...  78.2 us

profile of v5, /device:TPU:0, one launch (start us, length us, event | category | flops | bytes accessed | tf_op | source)
XLA Modules:
  0.0 79.0 jit_solution(5908918020670431390)
XLA Ops:
  0.0 78.2 %shard_map.46 = f32[640,128]{1,0:T(8,128)S(1)} custom-call(f32[1280,640]{1,0:T(8,128)} %green.1, f32[1280,128]{1,0:T(8,128)} %data.1, s32[3,640]{1,0:T(4,128)} %nb_in.1, f32[1,128]{1,0:T(1,128)} %bitcast.1), custom_call_target="tpu_custom_call" | custom-call | tf_op jit(solution)/shard_map/pallas_call | solution.py:875
  78.2 0.7 copy.6

commit v6 on v5

--- a/solution.py
+++ b/solution.py
@@ -38,7 +38,7 @@
            gbuf, gpar, dbuf, ghi, glo, nb, nbp, nbe, rw, lm, lmt,
            cat_d, cat_e, cat_u, lt, lt0,
            d, g, a, wown, wsrc, slip, slp, dp, sq, hsrc, hd, hg, qd, qg,
-           s, sr, sl, rl, rr, bb, br, nat, natp, hal, wr, scs, scr, zsq, pls, plr, tsrc, tdst,
+           s, sr, sl, rl, rr, bb, br, nat, natp, hal, wr, scs, scr, zsq, pls, plr, tsrc, tdst, acc_f, acc_b,
            sem_out, sem_l, sem_r, sem_b, sem_h, sem_w, sem_s, sem_p, sem_x, sem_y, sem_g, sem_nb, sem_in, sem_zs):
     rows, cols = gbuf.shape
     E = dbuf.shape[1]
@@ -237,9 +237,12 @@
             y = dot(lt0[...], ghi[:, pl.ds(c0, BAND)])
             y = y[:E] + y[E:] + dot(lt0[0:E, :], glo[:, pl.ds(c0, BAND)])
             return y.T
-        c0 = pl.multiple_of(m * 2 * BAND, 2 * BAND)
-        y = dot(lt[...], ghi[:, pl.ds(c0, 2 * BAND)])
-        y = y[:H] + y[H:] + dot(lt[0:H, :], glo[:, pl.ds(c0, 2 * BAND)])
+        c0 = m * 2 * BAND
+        if m == 0:
+            y = acc_b[...] + part_b(RB - 1)
+        else:
+            y = dot(lt[...], ghi[:, c0:c0 + 2 * BAND])
+            y = y[:H] + y[H:] + dot(lt[0:H, :], glo[:, c0:c0 + 2 * BAND])
         return jnp.concatenate([y[:, :BAND], y[:, BAND:]], axis=0).T
 
     def xcopy(m):
@@ -286,6 +289,7 @@
                 bb[b, p, j] = bb[b, p - 1, j] + br[b, p - 1, j]
                 bcopy(b, p, j).start()
 
+        acc_f[...] = jnp.zeros(acc_f.shape, F32)
         late()
 
         @pl.loop(0, bc)
@@ -307,6 +311,11 @@
 
     def hcopy_l(it):
         return rcopy(hsrc.at[it, 1], hal.at[it, 1], (sem_out.at[5], sem_h.at[it % 2, 1]), at(obs, pat - 2))
+
+    def part_b(m):
+        ks = pl.ds(pl.multiple_of(m * 2 * BAND, 2 * BAND), 2 * BAND)
+        y = dot(lt[:, ks], ghi[ks, 0:2 * BAND])
+        return y[:H] + y[H:] + dot(lt[0:H, ks], glo[ks, 0:2 * BAND])
 
     def put_lt(m):
         x = qd[pl.ds(m * per, per)].reshape(BAND, E)
@@ -318,6 +327,17 @@
         lt[0:H, pl.ds(o1, BAND)] = hi[H:]
         lt[H:E, pl.ds(o1, BAND)] = lo[H:]
 
+        @pl.when(m < RB - 1)
+        def _():
+            acc_b[...] += part_b(m)
+
+    def part_f(it, i):
+        m = jnp.where((it == ITERS - 1) & (z <= za), RB - 1, 0) if it == ITERS - 1 else 0
+        rs = pl.ds(pl.multiple_of(m * 2 * BAND, 2 * BAND), 2 * BAND) if it == ITERS - 1 else slice(0, 2 * BAND)
+        ks = pl.ds(pl.multiple_of(i * 2 * BAND, 2 * BAND), 2 * BAND)
+        y = dot(ghi[rs, ks], cat_d[ks, 0:2 * E])
+        return y[:, :E] + y[:, E:] + dot(glo[rs, ks], cat_d[ks, 2 * E:3 * E])
+
     def forward(it, sums, after, hook):
         last = it == ITERS - 1
         v = a if it else g
@@ -335,10 +355,15 @@
             forward_last(sums, hook)
             return
 
+        acc_b[...] = jnp.zeros(acc_b.shape, F32)
+
         def group(m):
             r0 = m * 2 * BAND
-            y = dot(ghi[r0:r0 + 2 * BAND, :], cat_d[:, 0:2 * E])
-            y = y[:, :E] + y[:, E:] + dot(glo[r0:r0 + 2 * BAND, :], cat_d[:, 2 * E:3 * E])
+            if m == 0:
+                y = acc_f[...] + part_f(it, CB - 1)
+            else:
+                y = dot(ghi[r0:r0 + 2 * BAND, :], cat_d[:, 0:2 * E])
+                y = y[:, :E] + y[:, E:] + dot(glo[r0:r0 + 2 * BAND, :], cat_d[:, 2 * E:3 * E])
             y = jnp.where(low(BAND), y[:BAND], y[BAND:])
             s[m * per:(m + 1) * per] = y.reshape(per, R, E)
 
@@ -431,8 +456,11 @@
         def group(i):
             m = order(i, RB)
             rs = pl.ds(pl.multiple_of(m * 2 * BAND, 2 * BAND), 2 * BAND)
-            y = dot(ghi[rs, :], cat_d[:, 0:2 * E])
-            y = y[:, :E] + y[:, E:] + dot(glo[rs, :], cat_d[:, 2 * E:3 * E])
+            if i == 0:
+                y = acc_f[...] + part_f(it, CB - 1)
+            else:
+                y = dot(ghi[rs, :], cat_d[:, 0:2 * E])
+                y = y[:, :E] + y[:, E:] + dot(glo[rs, :], cat_d[:, 2 * E:3 * E])
             y = jnp.where(low(BAND), y[:BAND], y[BAND:])
             s[pl.ds(m * per, per)] = y.reshape(per, R, E)
 
@@ -730,12 +758,16 @@
             def _(i):
                 put_green(gpar, i, other)
 
-    def put_operand(ref, i):
+    def put_operand(ref, i, it):
         top, bot = both(ref[pl.ds(pl.multiple_of(i * BAND, BAND), BAND), :])
         r0 = pl.multiple_of(i * 2 * BAND, 2 * BAND)
         put_cat(cat_d, r0, top, True)
         put_cat(cat_d, pl.multiple_of(r0 + BAND, BAND), bot, True)
 
+        @pl.when(i < CB - 1)
+        def _():
+            acc_f[...] += part_f(it, i)
+
     def first_finish(j, x):
         r0 = pl.multiple_of(j * R, R)
         g[pl.ds(r0, R), :] = x
@@ -743,7 +775,7 @@
 
         @pl.when(j % per == per - 1)
         def _():
-            put_operand(g, j // per)
+            put_operand(g, j // per, 0)
 
     backward(0, first_hook, first_late, first_finish)
     forward(0, lambda: None, lambda: pl.when(c == 1)(build_laplace), first)
@@ -755,13 +787,13 @@
             def _():
                 reg_work(it - 1)
 
-        def finish(j, x):
+        def finish(j, x, it=it):
             r0 = pl.multiple_of(j * R, R)
             a[pl.ds(r0, R), :] = x + wown[pl.ds(r0, R), :]
 
             @pl.when(j % per == per - 1)
             def _():
-                put_operand(a, j // per)
+                put_operand(a, j // per, it)
 
         backward(it, hook, functools.partial(reg_end, it - 1), finish)
         forward(it, functools.partial(dots, it - 1), lambda: None, functools.partial(advance, it))
@@ -869,6 +901,7 @@
         V((ITERS, 2, HB, E), F32), V((ITERS - 1, 2, HB, E), F32),
         V((ITERS, 8, E), F32), V((ITERS, nz, 8, E), F32),
         V((2, 8, E), F32), V((8, E), F32), V((2 * n_obs, 8, E), F32), V((8, E), F32), V((8, E), F32),
+        V((2 * BAND, E), F32), V((E // 2, 2 * BAND), F32),
         D((10,)), D((2, nc)), D((2, nc)), D((2, nbit, bc)), D((2, 2)), D((ITERS - 1, 2)),
         D((ITERS,)), D((4,)), D((cols // BAND,)), D((2, 3)), D((2,)), D((2,)), D((rows // (2 * BAND) + 3,)), D((1,)),
     ]

time: 79.1 us -> 78.4 us (level)
  no operation moved by 1% of the time
where the time goes in v6:
time: 78.4 us; the launch traced here: 78.2 us
  Pallas kernels  77.5 us (99%)
    pallas_call x1, Pallas kernels, shards(): pl.pallas_call(functools.partial(kernel, n_obs, n_patch, nc, bc), out_sha...  77.5 us

profile of v6, /device:TPU:0, one launch (start us, length us, event | category | flops | bytes accessed | tf_op | source)
XLA Modules:
  0.0 78.2 jit_solution(16334781741439761976)
XLA Ops:
  0.0 77.5 %shard_map.46 = f32[640,128]{1,0:T(8,128)S(1)} custom-call(f32[1280,640]{1,0:T(8,128)} %green.1, f32[1280,128]{1,0:T(8,128)} %data.1, s32[3,640]{1,0:T(4,128)} %nb_in.1, f32[1,128]{1,0:T(1,128)} %bitcast.1), custom_call_target="tpu_custom_call" | custom-call | tf_op jit(solution)/shard_map/pallas_call | solution.py:908
  77.5 0.7 copy.6

commit v7 on v6

--- a/solution.py
+++ b/solution.py
@@ -478,6 +478,10 @@
 
         group(0)
         send([0])
+        first, *others = batches(RB)[1:]
+        for i in first:
+            group(i)
+        send(first)
         sums()
 
         @pl.when(up & (z == 0))
@@ -488,7 +492,7 @@
         def _():
             hcopy_l(it).start()
 
-        for ms in batches(RB)[1:]:
+        for ms in others:
             for i in ms:
                 group(i)
             send(ms)

time: 78.4 us -> 78 us (level)
  no operation moved by 1% of the time
where the time goes in v7:
time: 78 us; the launch traced here: 77.8 us
  Pallas kernels  77.1 us (99%)
    pallas_call x1, Pallas kernels, shards(): pl.pallas_call(functools.partial(kernel, n_obs, n_patch, nc, bc), out_sha...  77.1 us

profile of v7, /device:TPU:0, one launch (start us, length us, event | category | flops | bytes accessed | tf_op | source)
XLA Modules:
  0.0 77.8 jit_solution(15114151660821704171)
XLA Ops:
  0.0 77.1 %shard_map.46 = f32[640,128]{1,0:T(8,128)S(1)} custom-call(f32[1280,640]{1,0:T(8,128)} %green.1, f32[1280,128]{1,0:T(8,128)} %data.1, s32[3,640]{1,0:T(4,128)} %nb_in.1, f32[1,128]{1,0:T(1,128)} %bitcast.1), custom_call_target="tpu_custom_call" | custom-call | tf_op jit(solution)/shard_map/pallas_call | solution.py:912
  77.1 0.7 copy.6
